TPU v7x, 32 devices: a 4x4x1 block of a 4x4x8 slice. The times are simulated.
32 devices in a mesh: dp: 1 (over z), tp: 32 (over y, x, core).
Axes of the slice: x: 4, y: 4, z: 1, core: 2. Of those that a mesh axis runs over, the one named last changes fastest.
The devices are a block of a 4x4x8 slice.
Arguments:
- hidden_in: bfloat16 [3, 1024, 4096], P('dp', 'tp')
- norms: float32 [2, 4, 4096], replicated
- w_qkv: bfloat16 [2, 4096, 3, 32, 128], P(None, None, None, 'tp')
- w_out: bfloat16 [2, 32, 128, 4096], P(None, 'tp')
- b_out: float32 [2, 4096], replicated
- w_up: bfloat16 [2, 4096, 16384], P(None, None, 'tp')
- b_up: float32 [2, 16384], P(None, 'tp')
- w_down: bfloat16 [2, 16384, 4096], P(None, 'tp')
- b_down: float32 [2, 4096], replicated
Outputs:
- output: bfloat16 [3, 1024, 4096], P('dp', 'tp')
All inputs are finite; a program needn't handle non-finite values.
Results may differ from a plain program's by a relative error of at most 0.0104407.
Values are sent between devices in bfloat16 or wider.
A program may use at most 768 MiB of HBM per device.

v0:
```python
import jax
import jax.numpy as jnp
from jax import lax
from jax.sharding import PartitionSpec as P

LN_EPS = 1e-5


def layer_norm(rows, gain, shift):
    row_mean = jnp.mean(rows, axis=-1, keepdims=True)
    centred = rows - row_mean
    row_var = jnp.mean(centred * centred, axis=-1, keepdims=True)
    return (centred * lax.rsqrt(row_var + LN_EPS) * gain + shift).astype(jnp.bfloat16)


def attention(qkv_rows, head_dim):
    scores = jnp.einsum('bqhe,bkhe->bhqk', qkv_rows[:, :, 0], qkv_rows[:, :, 1], preferred_element_type=jnp.float32) * head_dim ** -0.5
    attn_prob = jax.nn.softmax(scores, axis=-1).astype(jnp.bfloat16)
    return jnp.einsum('bhqk,bkhe->bqhe', attn_prob, qkv_rows[:, :, 2], preferred_element_type=jnp.float32).astype(jnp.bfloat16)


def reduce_rows(partial, group_size):
    batch_loc, seq_len, width = partial.shape
    received = lax.all_to_all(partial.astype(jnp.bfloat16), 'tp', 1, 0, tiled=True)
    received = received.reshape(group_size, batch_loc, seq_len // group_size, width)
    return jnp.sum(received.astype(jnp.float32), axis=0)


def solution(mesh):
    group_size = mesh.shape['tp']

    def local_layers(hidden_in, norms, w_qkv, w_out, b_out, w_up, b_up, w_down, b_down):
        head_dim = w_qkv.shape[-1]
        residual = hidden_in.astype(jnp.float32)
        for layer_idx in range(w_qkv.shape[0]):
            normed = layer_norm(residual, norms[layer_idx, 0], norms[layer_idx, 1])
            full_rows = lax.all_gather(normed, 'tp', axis=1, tiled=True)
            qkv_rows = jnp.einsum('bsd,dthe->bsthe', full_rows, w_qkv[layer_idx], preferred_element_type=jnp.float32).astype(jnp.bfloat16)
            attn_rows = attention(qkv_rows, head_dim)
            partial = jnp.einsum('bshe,hed->bsd', attn_rows, w_out[layer_idx], preferred_element_type=jnp.float32)
            residual = residual + reduce_rows(partial, group_size) + b_out[layer_idx]
            normed2 = layer_norm(residual, norms[layer_idx, 2], norms[layer_idx, 3])
            full_rows2 = lax.all_gather(normed2, 'tp', axis=1, tiled=True)
            hidden = jnp.einsum('bsd,df->bsf', full_rows2, w_up[layer_idx], preferred_element_type=jnp.float32) + b_up[layer_idx]
            gelu_out = jax.nn.gelu(hidden, approximate=True).astype(jnp.bfloat16)
            partial2 = jnp.einsum('bsf,fd->bsd', gelu_out, w_down[layer_idx], preferred_element_type=jnp.float32)
            residual = residual + reduce_rows(partial2, group_size) + b_down[layer_idx]
        return residual.astype(jnp.bfloat16)

    in_specs = (P('dp', 'tp', None), P(), P(None, None, None, 'tp', None), P(None, 'tp', None, None), P(), P(None, None, 'tp'), P(None, 'tp'), P(None, 'tp', None), P())
    return jax.shard_map(local_layers, mesh=mesh, in_specs=in_specs, out_specs=P('dp', 'tp', None), check_vma=False)
```

profile of v0, /device:TPU:96, one launch (start us, length us, event | category | flops | bytes accessed | tf_op | source)
XLA Modules:
  0.0 2513.5 jit_solution(1069272480588227560)
XLA Ops:
  13.7 89.4 %all-gather.5.cloned.1.call-done = bf16[3,1024,4096]{2,1,0:T(8,128)(2,1)} async-done(((bf16[3,32,4096]{2,1,0:T(8,128)(2,1)}), bf16[3,1024,4096]{2,1,0:T(8,128)(2,1)}) %all-gather.5.cloned.1.call-update) | async-done | bytes 25165840 | tf_op jit(solution)/shard_map/all_gather | solution.py:37
  103.1 19.9 convert_bitcast_fusion.1
  123.0 9.9 fusion.111
  132.9 17.1 convolution_convert_fusion.3
  149.9 35.8 %copy.34 = bf16[3,1024,4096]{2,0,1:T(4,128)(2,1)} copy(bf16[3,1024,4096]{2,1,0:T(8,128)(2,1)} %convolution_convert_fusion.3) | data formatting | bytes 50331648 | tf_op jit(solution)/shard_map/convert_element_type | solution.py:24
  185.7 5.2 all-to-all-start
  191.7 415.2 %all-to-all-done = bf16[3,1024,4096]{2,0,1:T(4,128)(2,1)} async-done(((bf16[3,1024,4096]{2,0,1:T(4,128)(2,1)}), bf16[3,1024,4096]{2,0,1:T(4,128)(2,1)}, u32[]{:S(2)}, u32[]{:S(2)}) %all-to-all-start) | async-done | bytes 25165856 | tf_op jit(solution)/shard_map/all_to_all | solution.py:24
  606.9 16.9 convert_reduce_fusion.3
  623.8 2.7 fusion.105
  628.8 123.4 %all-gather.7.cloned.1.call-done = bf16[3,1024,4096]{2,1,0:T(8,128)(2,1)} async-done(((bf16[3,32,4096]{2,1,0:T(8,128)(2,1)}), bf16[3,1024,4096]{2,1,0:T(8,128)(2,1)}) %all-gather.7.cloned.1.call-update) | async-done | bytes 25165840 | tf_op jit(solution)/shard_map/all_gather | solution.py:43
  752.2 22.2 fusion.19.clone.5
  774.4 21.0 convolution_convert_fusion.2
  795.4 35.6 %copy.36 = bf16[3,1024,4096]{2,0,1:T(4,128)(2,1)} copy(bf16[3,1024,4096]{2,1,0:T(8,128)(2,1)} %convolution_convert_fusion.2) | data formatting | bytes 50331648 | tf_op jit(solution)/shard_map/convert_element_type | solution.py:24
  830.9 5.2 all-to-all-start.1
  836.9 415.2 %all-to-all-done.1 = bf16[3,1024,4096]{2,0,1:T(4,128)(2,1)} async-done(((bf16[3,1024,4096]{2,0,1:T(4,128)(2,1)}), bf16[3,1024,4096]{2,0,1:T(4,128)(2,1)}, u32[]{:S(2)}, u32[]{:S(2)}) %all-to-all-start.1) | async-done | bytes 25165856 | tf_op jit(solution)/shard_map/all_to_all | solution.py:24
  1252.1 16.9 convert_reduce_fusion.2
  1269.1 2.6 fusion.103
  1273.4 124.0 %all-gather.9.cloned.1.call-done = bf16[3,1024,4096]{2,1,0:T(8,128)(2,1)} async-done(((bf16[3,32,4096]{2,1,0:T(8,128)(2,1)}), bf16[3,1024,4096]{2,1,0:T(8,128)(2,1)}) %all-gather.9.cloned.1.call-update) | async-done | bytes 25165840 | tf_op jit(solution)/shard_map/all_gather | solution.py:37
  1397.3 20.1 convert_bitcast_fusion
  1417.5 9.9 fusion.112
  1427.3 17.1 convolution_convert_fusion.1
  1444.4 35.8 %copy.42 = bf16[3,1024,4096]{2,0,1:T(4,128)(2,1)} copy(bf16[3,1024,4096]{2,1,0:T(8,128)(2,1)} %convolution_convert_fusion.1) | data formatting | bytes 50331648 | tf_op jit(solution)/shard_map/convert_element_type | solution.py:24
  1480.2 410.6 %all_to_all.16 = bf16[3,1024,4096]{2,0,1:T(4,128)(2,1)} all-to-all(bf16[3,1024,4096]{2,0,1:T(4,128)(2,1)} %copy.42), channel_id=1, replica_groups=mesh['dp'=1,'tp'=32] {'tp'}, dimensions={1} | all-to-all | bytes 50331648 | tf_op jit(solution)/shard_map/all_to_all | solution.py:24
  1890.8 17.0 convert_reduce_fusion.1
  1907.8 2.7 fusion.101
  1912.1 99.6 %all-gather.11.cloned.1.call-done = bf16[3,1024,4096]{2,1,0:T(8,128)(2,1)} async-done(((bf16[3,32,4096]{2,1,0:T(8,128)(2,1)}), bf16[3,1024,4096]{2,1,0:T(8,128)(2,1)}) %all-gather.11.cloned.1.call-update) | async-done | bytes 25165840 | tf_op jit(solution)/shard_map/all_gather | solution.py:43
  2011.7 22.1 fusion.27.clone.5
  2033.8 20.8 convolution_convert_fusion
  2054.6 35.6 %copy.44 = bf16[3,1024,4096]{2,0,1:T(4,128)(2,1)} copy(bf16[3,1024,4096]{2,1,0:T(8,128)(2,1)} %convolution_convert_fusion) | data formatting | bytes 50331648 | tf_op jit(solution)/shard_map/convert_element_type | solution.py:24
  2090.2 396.0 %all_to_all.17 = bf16[3,1024,4096]{2,0,1:T(4,128)(2,1)} all-to-all(bf16[3,1024,4096]{2,0,1:T(4,128)(2,1)} %copy.44), channel_id=1, replica_groups=mesh['dp'=1,'tp'=32] {'tp'}, dimensions={1} | all-to-all | bytes 50331648 | tf_op jit(solution)/shard_map/all_to_all | solution.py:24
  2486.2 17.0 convert_reduce_fusion
  2503.1 3.4 fusion.78
  (51 shorter events, 14.0 us)
Async XLA Ops:
  6.5 96.5 %all-gather.5.cloned.1.call-start = ((), (), s32[]{:S(2)}) async-start(), calls=%async_computation.4 | async-start | bytes 25952256 | tf_op jit(solution)/shard_map/all_gather | solution.py:37
  185.7 5.3 copy-start.7
  185.7 421.2 %all-to-all-start = ((bf16[3,1024,4096]{2,0,1:T(4,128)(2,1)}), bf16[3,1024,4096]{2,0,1:T(4,128)(2,1)}, u32[]{:S(2)}, u32[]{:S(2)}) async-start(bf16[3,1024,4096]{2,0,1:T(4,128)(2,1)} %copy.34), calls=%async_computation | async-start | bytes 67108864 | tf_op jit(solution)/shard_map/all_to_all | solution.py:24
  191.0 561.2 %all-gather.7.cloned.1.call-start = ((), (), s32[]{:S(2)}) async-start(), calls=%async_computation.5 | async-start | bytes 25952256 | tf_op jit(solution)/shard_map/all_gather | solution.py:43
  606.9 16.9 copy-start
  623.8 4.3 copy-start.9
  830.9 5.3 copy-start.8
  830.9 421.2 %all-to-all-start.1 = ((bf16[3,1024,4096]{2,0,1:T(4,128)(2,1)}), bf16[3,1024,4096]{2,0,1:T(4,128)(2,1)}, u32[]{:S(2)}, u32[]{:S(2)}) async-start(bf16[3,1024,4096]{2,0,1:T(4,128)(2,1)} %copy.36), calls=%async_computation.1 | async-start | bytes 67108864 | tf_op jit(solution)/shard_map/all_to_all | solution.py:24
  836.2 561.2 %all-gather.9.cloned.1.call-start = ((), (), s32[]{:S(2)}) async-start(), calls=%async_computation.6 | async-start | bytes 25952256 | tf_op jit(solution)/shard_map/all_gather | solution.py:37
  1269.1 3.0 copy-start.3
  1269.1 3.0 copy-start.4
  1273.3 738.4 %all-gather.11.cloned.1.call-start = ((), (), s32[]{:S(2)}) async-start(), calls=%async_computation.7 | async-start | bytes 25952256 | tf_op jit(solution)/shard_map/all_gather | solution.py:43
  1890.8 17.0 copy-start.5
  1907.8 3.0 copy-start.1
  1907.8 3.0 copy-start.2
  1907.8 103.9 %copy-start.10 = (f32[1,512]{1,0:T(1,128)S(1)}, f32[1,512]{1,0:T(1,128)}, u32[]{:S(2)}) copy-start(f32[1,512]{1,0:T(1,128)} %get-tuple-element.23) | copy-start | bytes 6148
  2486.2 17.0 copy-start.6
Sparse Core Ops, SparseCore 0:
  13.9 89.1 all-gather.4
  628.3 123.8 all-gather.6
  1273.4 123.8 all-gather.8
  1912.2 99.4 all-gather.10
where the time goes:
time: 2550 us; the launch traced here: 2510 us
  waiting for transfers between devices  1270 us (50%)
  blocking collectives  807 us (32%)
  matrix products  180 us (7%)
  local copies, waits for them, and re-layouts  147 us (6%)
  other arithmetic  89 us (3%)
    all_to_all x2, waiting for transfers between devices, reduce_rows(): lax.all_to_all(partial.astype(jnp.bfloat16), 'tp', 1, 0, tiled=True)  830 us
    all_to_all x2, blocking collectives, reduce_rows(): lax.all_to_all(partial.astype(jnp.bfloat16), 'tp', 1, 0, tiled=True)  807 us
    all_gather x2, waiting for transfers between devices, local_layers(): full_rows2 = lax.all_gather(normed2, 'tp', axis=1, tiled=True)  223 us
    all_gather x2, waiting for transfers between devices, local_layers(): full_rows = lax.all_gather(normed, 'tp', axis=1, tiled=True)  213 us
    convert_element_type x4, local copies, waits for them, and re-layouts, reduce_rows(): partial.astype(jnp.bfloat16)  143 us
    reduce_sum x4, other arithmetic, reduce_rows(): return jnp.sum(received.astype(jnp.float32), axis=0)  67.8 us
  transfers between devices with their start and end apart: 6, of which 6 were waited for; matrix products, arithmetic and copies ran while one was open for 0% of the time, Pallas kernels for 0%

commit v1 on v0

v1 whole, which is shorter than its diff:
```python
import functools
import math

import jax
import jax.numpy as jnp
from jax import lax
from jax.experimental import pallas as pl
from jax.experimental.pallas import tpu as pltpu
from jax.sharding import PartitionSpec as P

LN_EPS = 1e-5
MESH = pl.DeviceIdType.MESH
F32 = jnp.float32
BF16 = jnp.bfloat16
VMEM_LIMIT = 66_900_000
TILE = 16


class Place:
    def __init__(self, group_size):
        self.side = side = math.isqrt(group_size // 2)
        self.chips = side * side
        index = lax.axis_index("tp")
        self.core = index % 2
        chip = index // 2
        x, y = chip % side, chip // side
        self.first = x * (1 - self.core) + y * self.core
        self.second = y * (1 - self.core) + x * self.core
        self.pos = self.pos_of(self.first, self.second)

    def device(self, first, second):
        x = first * (1 - self.core) + second * self.core
        y = second * (1 - self.core) + first * self.core
        return {"tp": (y * self.side + x) * 2 + self.core}

    def partner(self):
        x = self.first * (1 - self.core) + self.second * self.core
        y = self.second * (1 - self.core) + self.first * self.core
        return {"tp": (y * self.side + x) * 2 + 1 - self.core}

    def pos_of(self, first, second):
        return second * self.side + (first + second) % self.side

    def at_pos(self, pos):
        second = pos // self.side
        return (pos % self.side + self.side - second) % self.side, second

    def barrier(self):
        barrier = pltpu.get_barrier_semaphore()
        peers = [self.device((self.first + d) % self.side, self.second) for d in range(1, self.side)]
        peers += [self.device(self.first, (self.second + d) % self.side) for d in range(1, self.side)]
        peers.append(self.partner())
        for peer in peers:
            pl.semaphore_signal(barrier, inc=1, device_id=peer, device_id_type=MESH)
        pl.semaphore_wait(barrier, len(peers))


def far_first(side):
    return sorted(range(1, side), key=lambda d: -min(d, side - d))


def remote(src, dst, send_sem, recv_sem, device):
    return pltpu.make_async_remote_copy(src_ref=src, dst_ref=dst, send_sem=send_sem, recv_sem=recv_sem, device_id=device, device_id_type=MESH)


def norm_rows(r_ref, gain, shift, buf):
    def rows_of(i, carry):
        rows = pl.ds(pl.multiple_of(i * TILE, TILE), TILE)
        v = r_ref[rows, :]
        mean = jnp.mean(v, axis=-1, keepdims=True)
        v = v - mean
        var = jnp.mean(v * v, axis=-1, keepdims=True)
        buf[0, rows, :] = (v * lax.rsqrt(var + LN_EPS) * gain + shift).astype(BF16)
        return carry
    lax.fori_loop(0, r_ref.shape[0] // TILE, rows_of, 0)


class Gather:
    def __init__(self, place, buf, send, recv):
        self.place, self.buf, self.send, self.recv = place, buf, send, recv
        self.half = buf.shape[1] // 2
        self.subs = self.half // TILE
        n = place.chips
        self.next = [place.device(*place.at_pos((place.pos + 1) % n)), place.device(*place.at_pos((place.pos + n - 1) % n))]

    def hop(self, dr, s, k):
        rows = pl.ds(dr * self.half + k * TILE, TILE)
        return remote(self.buf.at[s, rows], self.buf.at[s + 1, rows], self.send.at[dr, s, k], self.recv.at[dr, s, k], self.next[dr])

    def start(self):
        for k in range(self.subs):
            for dr in range(2):
                self.hop(dr, 0, k).start()

    def take(self, s, k):
        for dr in range(2):
            self.hop(dr, s - 1, k).wait_recv()

            @pl.when(s < self.place.chips - 1)
            def _():
                self.hop(dr, s, k).start()

    def sent(self, s):
        @pl.when(s < self.place.chips - 1)
        def _():
            for dr in range(2):
                for k in range(self.subs):
                    self.hop(dr, s, k).wait_send()

    def run(self, part):
        n = self.place.chips // 2
        for k in range(self.subs):
            self.take(1, k)

        def step(j, carry):
            for h in range(2):
                for k in range(self.subs):
                    self.take(2 * j + h, k)
                    part(j - 1, h * self.subs + k)
            return carry
        lax.fori_loop(1, n, step, 0)
        for i in range(2 * self.subs):
            part(n - 1, i)


class Scatter:
    def __init__(self, place, buf, r1, sums, r2, s1_send, s1_recv, s2_send, s2_recv):
        self.place, self.buf, self.r1, self.sums, self.r2 = place, buf, r1, sums, r2
        self.s1_send, self.s1_recv, self.s2_send, self.s2_recv = s1_send, s1_recv, s2_send, s2_recv
        self.half = buf.shape[1] // 2

    def rows(self, dr):
        return pl.ds(dr * self.half, self.half)

    def first_copy(self, slot, dr, j, first, second):
        p = self.place
        return remote(self.buf.at[slot, self.rows(dr)], self.r1.at[j, second, self.rows(dr)], self.s1_send.at[j, second, dr],
                      self.s1_recv.at[j, second, dr], p.device(first, p.second))

    def send_slot(self, slot):
        p = self.place
        for dr in range(2):
            pos = (p.pos + (p.chips - slot if dr == 0 else slot)) % p.chips
            first, second = p.at_pos(pos)
            away = (first + p.side - p.first) % p.side

            @pl.when(away != 0)
            def _():
                self.first_copy(slot, dr, p.side - 1 - away, first, second).start()

    def slot_of(self, first, second, dr):
        p = self.place
        pos = p.pos_of(first, second)
        return (p.pos + p.chips - pos) % p.chips if dr == 0 else (pos + p.chips - p.pos) % p.chips

    def send_owner(self, away, second, dr):
        p = self.place
        first = (p.first + away) % p.side
        self.first_copy(self.slot_of(first, second, dr), dr, p.side - 1 - away, first, second).start()

    def second_copy(self, d, dr):
        p = self.place
        return remote(self.sums.at[d - 1, self.rows(dr)], self.r2.at[p.side - 1 - d, self.rows(dr)], self.s2_send.at[p.side - 1 - d, dr],
                      self.s2_recv.at[p.side - 1 - d, dr], p.device(p.first, (p.second + d) % p.side))

    def finish(self, r_ref, bias_ref, out_ref):
        p = self.place
        peers = range(p.side - 1)

        def arrived(second, dr):
            for j in peers:
                self.first_copy(0, dr, j, p.first, second).wait_recv()

        def total(second, dr, rows):
            v = self.buf[self.slot_of(p.first, second, dr), rows, :].astype(F32)
            for j in peers:
                v = v + self.r1[j, second, rows, :].astype(F32)
            return v

        def each(dr, fn):
            def one(i, carry):
                fn(pl.ds(pl.multiple_of(dr * self.half + i * TILE, TILE), TILE))
                return carry
            lax.fori_loop(0, self.half // TILE, one, 0)

        for d in far_first(p.side):
            second = (p.second + d) % p.side
            for dr in range(2):
                arrived(second, dr)

                def store(rows):
                    self.sums[d - 1, rows, :] = total(second, dr, rows)
                each(dr, store)
                self.second_copy(d, dr).start()
        for dr in range(2):
            arrived(p.second, dr)
            for d in range(1, p.side):
                self.second_copy(d, dr).wait_recv()

            def last(rows):
                v = total(p.second, dr, rows)
                for j in peers:
                    v = v + self.r2[j, rows, :]
                out_ref[rows, :] = (r_ref[rows, :] + v + bias_ref[...]).astype(out_ref.dtype)
            each(dr, last)
        for dr in range(2):
            for j in peers:
                for second in range(p.side):
                    self.first_copy(0, dr, j, p.first, second).wait_send()
            for d in range(1, p.side):
                self.second_copy(d, dr).wait_send()


class Share:
    def __init__(self, place, pairs, local, send, recv):
        self.place, self.pairs, self.local, self.send, self.recv = place, pairs, local, send, recv

    def load(self, i):
        src, own, _ = self.pairs[i]
        return pltpu.make_async_copy(src, own, self.local.at[i])

    def give(self, i):
        _, own, other = self.pairs[i]
        return remote(own, other, self.send.at[i], self.recv.at[i], self.place.partner())


def attn_kernel(group_size, layer, head_dim, n_seq, r_ref, norm_ref, bias_ref, wqkv_ref, wout_ref, out_ref,
                buf, w, wo, qkv, kvp, att, r1, sums, r2, wl, ws, wr, ag_send, ag_recv, kv_send, kv_recv, s1_send, s1_recv, s2_send, s2_recv):
    place = Place(group_size)
    hd = head_dim
    slots, block = buf.shape[0], buf.shape[1]
    per_seq = block // n_seq
    share = Share(place, [(wqkv_ref.at[layer], w.at[:, pl.ds(0, 3 * hd)], w.at[:, pl.ds(3 * hd, 3 * hd)]),
                          (wout_ref.at[layer], wo.at[pl.ds(0, hd)], wo.at[pl.ds(hd, hd)])], wl, ws, wr)
    for i in range(2):
        share.load(i).start()
    norm_rows(r_ref, norm_ref[0:1, :], norm_ref[1:2, :], buf)
    place.barrier()
    gather = Gather(place, buf, ag_send, ag_recv)
    gather.start()
    for i in range(2):
        share.load(i).wait()
        share.give(i).start()

    def kv_copy(j, h):
        pair = pl.ds(2 * j, 2)
        return remote(qkv.at[pair, :, pl.ds(3 * hd * h + hd, 2 * hd)], kvp.at[pair, :, pl.ds(2 * hd * (1 - h), 2 * hd)],
                      kv_send.at[j, h], kv_recv.at[j, h], place.partner())

    wide = 6 * hd // 3

    def part(j, i):
        if i % 2 == 0:
            if i == 0:
                @pl.when(j == 0)
                def _():
                    share.give(0).wait_recv()
            cols = pl.ds(i // 2 * wide, wide)
            rows = buf[pl.ds(2 * j, 2)].reshape(2 * block, buf.shape[2])
            qkv[pl.ds(2 * j, 2), :, cols] = jnp.dot(rows, w[:, cols], preferred_element_type=F32).astype(BF16).reshape(2, block, wide)
        if i == 5:
            for h in range(2):
                kv_copy(j, h).start()
            gather.sent(2 * j)
            gather.sent(2 * j + 1)
    gather.run(part)
    for j in range(slots // 2):
        for h in range(2):
            kv_copy(j, h).wait_recv()

    q_slots = slots // 2
    nq, nk = q_slots * per_seq, slots * per_seq

    def head_of(i, carry):
        seq, h, qi = i // 4, i // 2 % 2, i % 2
        rows = pl.ds(pl.multiple_of(seq * per_seq, per_seq), per_seq)
        at = pl.ds(pl.multiple_of(qi * q_slots, q_slots), q_slots)

        def cols(base, width, k):
            return pl.ds(pl.multiple_of(h * width + k * hd, hd), hd)
        q = qkv[at, rows, cols(0, 3 * hd, 0)].reshape(nq, hd)
        k0 = qkv[:, rows, cols(0, 3 * hd, 1)].reshape(nk, hd)
        v0 = qkv[:, rows, cols(0, 3 * hd, 2)].reshape(nk, hd)
        k1 = kvp[:, rows, cols(0, 2 * hd, 0)].reshape(nk, hd)
        v1 = kvp[:, rows, cols(0, 2 * hd, 1)].reshape(nk, hd)
        dims = (((1,), (1,)), ((), ()))
        s0 = lax.dot_general(q, k0, dims, preferred_element_type=F32) * hd ** -0.5
        s1 = lax.dot_general(q, k1, dims, preferred_element_type=F32) * hd ** -0.5
        top = jnp.maximum(jnp.max(s0, axis=-1, keepdims=True), jnp.max(s1, axis=-1, keepdims=True))
        e0 = jnp.exp(s0 - top)
        e1 = jnp.exp(s1 - top)
        inv = 1.0 / (jnp.sum(e0, axis=-1, keepdims=True) + jnp.sum(e1, axis=-1, keepdims=True))
        a = jnp.dot((e0 * inv).astype(BF16), v0, preferred_element_type=F32)
        a = a + jnp.dot((e1 * inv).astype(BF16), v1, preferred_element_type=F32)
        att[at, rows, pl.ds(pl.multiple_of(h * hd, hd), hd)] = a.astype(BF16).reshape(q_slots, per_seq, hd)
        return carry
    lax.fori_loop(0, n_seq * 4, head_of, 0)

    share.give(1).wait_recv()
    scatter = Scatter(place, buf, r1, sums, r2, s1_send, s1_recv, s2_send, s2_recv)
    width = buf.shape[2] // 4

    def project(i, carry):
        j, c = i // 4, i % 4
        rows = att[pl.ds(2 * j, 2)].reshape(2 * block, 2 * hd)
        cols = pl.ds(pl.multiple_of(c * width, width), width)
        buf[pl.ds(2 * j, 2), :, cols] = jnp.dot(rows, wo[:, cols], preferred_element_type=F32).astype(BF16).reshape(2, block, width)
        return carry
    lax.fori_loop(0, slots * 2, project, 0)
    for d in (*far_first(place.side), 0):
        for away in far_first(place.side):
            for dr in range(2):
                scatter.send_owner(away, (place.second + d) % place.side, dr)
    scatter.finish(r_ref, bias_ref, out_ref)
    for i in range(2):
        share.give(i).wait_send()
    for j in range(slots // 2):
        for h in range(2):
            kv_copy(j, h).wait_send()


def mlp_kernel(group_size, layer, r_ref, norm_ref, bias_ref, bup_ref, wup_ref, wdown_ref, out_ref,
               buf, wu, wd, bu, u, r1, sums, r2, wl, ws, wr, ag_send, ag_recv, s1_send, s1_recv, s2_send, s2_recv):
    place = Place(group_size)
    slots, block, model = buf.shape
    ff = wup_ref.shape[2]
    share = Share(place, [(bup_ref.at[pl.ds(layer, 1)], bu.at[:, pl.ds(0, ff)], bu.at[:, pl.ds(ff, ff)]),
                          (wup_ref.at[layer], wu.at[:, pl.ds(0, ff)], wu.at[:, pl.ds(ff, ff)]),
                          (wdown_ref.at[layer], wd.at[pl.ds(0, ff)], wd.at[pl.ds(ff, ff)])], wl, ws, wr)
    for i in range(3):
        share.load(i).start()
    norm_rows(r_ref, norm_ref[2:3, :], norm_ref[3:4, :], buf)
    place.barrier()
    gather = Gather(place, buf, ag_send, ag_recv)
    gather.start()
    for i in range(3):
        share.load(i).wait()
        share.give(i).start()
    scatter = Scatter(place, buf, r1, sums, r2, s1_send, s1_recv, s2_send, s2_recv)
    up_w, down_w = ff // 2, model // 4

    def up(j, c):
        rows = buf[pl.ds(2 * j, 2)].reshape(2 * block, model)
        cols = pl.ds(c * up_w, up_w)
        hidden = jnp.dot(rows, wu[:, cols], preferred_element_type=F32) + bu[:, cols]
        u[:, cols] = jax.nn.gelu(hidden, approximate=True).astype(BF16)

    def down(j, c):
        cols = pl.ds(c * down_w, down_w)
        buf[pl.ds(2 * j, 2), :, cols] = jnp.dot(u[...], wd[:, cols], preferred_element_type=F32).astype(BF16).reshape(2, block, down_w)

    def part(j, i):
        if i == 0:
            @pl.when(j == 0)
            def _():
                share.give(0).wait_recv()
                share.give(1).wait_recv()
            up(j, 0)
            up(j, 1)
        elif i == 1:
            up(j, 2)
        elif i == 2:
            up(j, 3)
        elif i == 3:
            @pl.when(j == 0)
            def _():
                share.give(2).wait_recv()
            gather.sent(2 * j)
            gather.sent(2 * j + 1)
            down(j, 0)
        elif i == 4:
            down(j, 1)
        else:
            down(j, 2)
            down(j, 3)
            scatter.send_slot(2 * j)
            scatter.send_slot(2 * j + 1)
    gather.run(part)
    scatter.finish(r_ref, bias_ref, out_ref)
    for i in range(3):
        share.give(i).wait_send()


def solution(mesh):
    group_size = mesh.shape["tp"]
    side = math.isqrt(group_size // 2)
    chips = side * side
    dma = pltpu.SemaphoreType.DMA
    vmem = pl.BlockSpec(memory_space=pltpu.VMEM)
    hbm = pl.BlockSpec(memory_space=pl.ANY)

    def local_layers(hidden_in, norms, w_qkv, w_out, b_out, w_up, b_up, w_down, b_down):
        n_seq, per_seq, model = hidden_in.shape
        n_layers, head_dim, ff = w_qkv.shape[0], w_qkv.shape[-1], w_up.shape[-1]
        block = n_seq * per_seq
        subs = block // 2 // TILE
        residual = hidden_in.astype(F32).reshape(block, model)
        w_qkv = w_qkv.reshape(n_layers, model, 3 * head_dim)
        w_out = w_out.reshape(n_layers, head_dim, model)
        ring = [dma((2, chips - 1, subs))] * 2
        reduce_bufs = [pltpu.VMEM((side - 1, side, block, model), BF16), pltpu.VMEM((side - 1, block, model), F32),
                       pltpu.VMEM((side - 1, block, model), F32)]
        reduce_sems = [dma((side - 1, side, 2))] * 2 + [dma((side - 1, 2))] * 2
        rows = pltpu.VMEM((chips, block, model), BF16)

        def params(collective_id):
            return pltpu.CompilerParams(collective_id=collective_id, has_side_effects=True, vmem_limit_bytes=VMEM_LIMIT)

        for layer in range(n_layers):
            residual = pl.pallas_call(
                functools.partial(attn_kernel, group_size, layer, head_dim, n_seq), name=f"attn{layer}",
                out_shape=jax.ShapeDtypeStruct((block, model), F32),
                in_specs=[vmem, vmem, vmem, hbm, hbm], out_specs=vmem,
                scratch_shapes=[rows, pltpu.VMEM((model, 6 * head_dim), BF16), pltpu.VMEM((2 * head_dim, model), BF16),
                                pltpu.VMEM((chips, block, 6 * head_dim), BF16), pltpu.VMEM((chips, block, 4 * head_dim), BF16),
                                pltpu.VMEM((chips, block, 2 * head_dim), BF16), *reduce_bufs, dma((2,)), dma((2,)), dma((2,)), *ring,
                                dma((chips // 2, 2)), dma((chips // 2, 2)), *reduce_sems],
                compiler_params=params(2 * layer),
            )(residual, norms[layer], b_out[layer][None], w_qkv, w_out)
            residual = pl.pallas_call(
                functools.partial(mlp_kernel, group_size, layer), name=f"mlp{layer}",
                out_shape=jax.ShapeDtypeStruct((block, model), F32 if layer < n_layers - 1 else BF16),
                in_specs=[vmem, vmem, vmem, hbm, hbm, hbm], out_specs=vmem,
                scratch_shapes=[rows, pltpu.VMEM((model, 2 * ff), BF16), pltpu.VMEM((2 * ff, model), BF16), pltpu.VMEM((1, 2 * ff), F32),
                                pltpu.VMEM((2 * block, 2 * ff), BF16), *reduce_bufs, dma((3,)), dma((3,)), dma((3,)), *ring, *reduce_sems],
                compiler_params=params(2 * layer + 1),
            )(residual, norms[layer], b_down[layer][None], b_up, w_up, w_down)
        return residual.reshape(n_seq, per_seq, model)

    in_specs = (P('dp', 'tp', None), P(), P(None, None, None, 'tp', None), P(None, 'tp', None, None), P(), P(None, None, 'tp'), P(None, 'tp'), P(None, 'tp', None), P())
    return jax.shard_map(local_layers, mesh=mesh, in_specs=in_specs, out_specs=P('dp', 'tp', None), check_vma=False)
```

time: 2550 us -> 858 us (0.34); the launches traced: 2510 us -> 857 us
  waiting for transfers between devices: 1270 us -> 0 us
  Pallas kernels: 0 us -> 834 us
  blocking collectives: 807 us -> 0 us
  matrix products: 180 us -> 0 us
  local copies, waits for them, and re-layouts: 147 us -> 22.1 us
  other arithmetic: 89 us -> 1.42 us
    pallas_call x0 -> x4, Pallas kernels: none -> 834 us  [the longest x2 428 us: local_layers(): pl.pallas_call(functools.partial(mlp_kernel, group_size, layer), name=f'm...]
    all_to_all x2 -> x0, waiting for transfers between devices: 830 us -> none  [reduce_rows(): lax.all_to_all(partial.astype(jnp.bfloat16), 'tp', 1, 0, tiled=True)]
    all_to_all x2 -> x0, blocking collectives: 807 us -> none  [reduce_rows(): lax.all_to_all(partial.astype(jnp.bfloat16), 'tp', 1, 0, tiled=True)]
    all_gather x4 -> x0, waiting for transfers between devices: 436 us -> none  [the longest x2 223 us: local_layers(): full_rows2 = lax.all_gather(normed2, 'tp', axis=1, tiled=True)]
    dot_general x8 -> x0, matrix products: 160 us -> none  [the longest x2 44.3 us: local_layers(): jnp.einsum('bsd,df->bsf', full_rows2, w_up[layer_idx], preferred_element_...]
    convert_element_type x4 -> x0, local copies, waits for them, and re-layouts: 143 us -> none  [reduce_rows(): partial.astype(jnp.bfloat16)]
    reduce_sum x12 -> x0, other arithmetic: 79.6 us -> none  [the longest x4 67.8 us: reduce_rows(): return jnp.sum(received.astype(jnp.float32), axis=0)]
  transfers between devices with their start and end apart: 6 -> 0, of which waited for: 6 -> 0; matrix products, arithmetic and copies ran while one was open for 0% -> 0% of each run, Pallas kernels for 0% -> 0%
where the time goes in v1:
time: 858 us; the launch traced here: 857 us
  Pallas kernels  834 us (97%)
  local copies, waits for them, and re-layouts  22.1 us (3%)
    pallas_call x2, Pallas kernels, local_layers(): pl.pallas_call(functools.partial(mlp_kernel, group_size, layer), name=f'm...  428 us
    pallas_call x2, Pallas kernels, local_layers(): pl.pallas_call(functools.partial(attn_kernel, group_size, layer, head_dim...  405 us

profile of v1, /device:TPU:96, one launch (start us, length us, event | category | flops | bytes accessed | tf_op | source)
XLA Modules:
  0.0 857.1 jit_solution(368146612948540920)
XLA Ops:
  0.0 1.5 slice_bitcast_fusion
  1.5 8.6 %copy.11 = bf16[2,4096,3,1,128]{1,4,2,0,3:T(8,128)(2,1)} copy(bf16[2,4096,3,1,128]{4,1,3,2,0:T(8,128)(2,1)} %param.11) | data formatting | bytes 12582912 | tf_op args[2]
  10.1 0.0 copy-start.1
  10.1 0.0 copy-start
  10.1 8.7 %copy.12.wqkv_ref = bf16[2,4096,384]{2,1,0:T(8,128)(2,1)} copy(bf16[2,4096,384]{1,2,0:T(8,128)(2,1)} %bitcast.10) | data formatting | bytes 12582912 | tf_op jit(solution)/shard_map/reshape | solution.py:398
  18.8 0.0 copy-done.1
  18.8 0.6 fusion.1
  19.4 0.0 copy-done
  19.4 1.4 bitcast_convert_fusion.r_ref
  20.9 0.0 copy-start.2
  20.9 204.5 %attn0.1.r_ref = f32[96,4096]{1,0:T(8,128)} custom-call(f32[96,4096]{1,0:T(8,128)} %bitcast_convert_fusion.r_ref, f32[4,4096]{1,0:T(4,128)} %get-tuple-element.6.norm_ref, f32[1,4096]{1,0:T(1,128)} %get-tuple-element.10.bias_ref, bf16[2,4096,384]{2,1,0:T(8,128)(2,1)} %copy.12.wqkv_ref, bf16[2,128,4096]{2,1,0:T(8,128)(2,1)} %bitcast.11), custom_call_target="tpu_custom_call" | custom-call | tf_op jit(solution)/shard_map/attn0/pallas_call | solution.py:410
  225.4 0.0 copy-done.2
  225.4 0.6 fusion
  226.1 214.3 %mlp0.1.r_ref = f32[96,4096]{1,0:T(8,128)} custom-call(f32[96,4096]{1,0:T(8,128)} %attn0.1.r_ref, f32[4,4096]{1,0:T(4,128)} %get-tuple-element.6.norm_ref, f32[1,4096]{1,0:T(1,128)} %get-tuple-element.8.bias_ref, f32[2,512]{1,0:T(2,128)} %bup_ref.3, bf16[2,4096,512]{2,1,0:T(8,128)(2,1)} %wup_ref.3, bf16[2,512,4096]{2,1,0:T(8,128)(2,1)} %wdown_ref.3), custom_call_target="tpu_custom_call" | custom-call | tf_op jit(solution)/shard_map/mlp0/pallas_call | solution.py:420
  440.4 200.7 %attn1.1.r_ref = f32[96,4096]{1,0:T(8,128)} custom-call(f32[96,4096]{1,0:T(8,128)} %mlp0.1.r_ref, f32[4,4096]{1,0:T(4,128)} %get-tuple-element.5.norm_ref, f32[1,4096]{1,0:T(1,128)} %get-tuple-element.9.bias_ref, bf16[2,4096,384]{2,1,0:T(8,128)(2,1)} %copy.12.wqkv_ref, bf16[2,128,4096]{2,1,0:T(8,128)(2,1)} %bitcast.12), custom_call_target="tpu_custom_call" | custom-call | tf_op jit(solution)/shard_map/attn1/pallas_call | solution.py:410
  641.1 214.0 %mlp1.1 = bf16[96,4096]{1,0:T(8,128)(2,1)} custom-call(f32[96,4096]{1,0:T(8,128)} %attn1.1.r_ref, f32[4,4096]{1,0:T(4,128)} %get-tuple-element.5.norm_ref, f32[1,4096]{1,0:T(1,128)} %get-tuple-element.7.bias_ref, f32[2,512]{1,0:T(2,128)} %bup_ref.3, bf16[2,4096,512]{2,1,0:T(8,128)(2,1)} %wup_ref.3, bf16[2,512,4096]{2,1,0:T(8,128)(2,1)} %wdown_ref.3), custom_call_target="tpu_custom_call" | custom-call | tf_op jit(solution)/shard_map/mlp1/pallas_call | solution.py:420
  855.1 2.1 copy.15
Async XLA Ops:
  10.1 8.7 %copy-start.1 = (f32[2,4096]{1,0:T(2,128)S(1)}, f32[2,4096]{1,0:T(2,128)}, u32[]{:S(2)}) copy-start(f32[2,4096]{1,0:T(2,128)} %param.13) | copy-start | bytes 98308
  10.1 9.3 %copy-start = (bf16[3,32,4096]{2,1,0:T(8,128)(2,1)S(1)}, bf16[3,32,4096]{2,1,0:T(8,128)(2,1)}, u32[]{:S(2)}) copy-start(bf16[3,32,4096]{2,1,0:T(8,128)(2,1)} %param.9) | copy-start | bytes 2359300
  20.9 204.5 %copy-start.2 = (f32[2,4096]{1,0:T(2,128)S(1)}, f32[2,4096]{1,0:T(2,128)}, u32[]{:S(2)}) copy-start(f32[2,4096]{1,0:T(2,128)} %param.17) | copy-start | bytes 98308

commit v2 on v1

v2 whole, which is shorter than its diff:
```python
import functools
import math

import jax
import jax.numpy as jnp
from jax import lax
from jax.experimental import pallas as pl
from jax.experimental.pallas import tpu as pltpu
from jax.sharding import PartitionSpec as P

LN_EPS = 1e-5
MESH = pl.DeviceIdType.MESH
F32 = jnp.float32
BF16 = jnp.bfloat16
VMEM_LIMIT = 66_900_000
TILE = 16


class Place:
    def __init__(self, group_size):
        self.side = side = math.isqrt(group_size // 2)
        self.chips = side * side
        index = lax.axis_index("tp")
        self.core = index % 2
        chip = index // 2
        x, y = chip % side, chip // side
        self.first = x * (1 - self.core) + y * self.core
        self.second = y * (1 - self.core) + x * self.core
        self.pos = self.pos_of(self.first, self.second)

    def device(self, first, second):
        x = first * (1 - self.core) + second * self.core
        y = second * (1 - self.core) + first * self.core
        return {"tp": (y * self.side + x) * 2 + self.core}

    def partner(self):
        x = self.first * (1 - self.core) + self.second * self.core
        y = self.second * (1 - self.core) + self.first * self.core
        return {"tp": (y * self.side + x) * 2 + 1 - self.core}

    def pos_of(self, first, second):
        return second * self.side + (first + second) % self.side

    def at_pos(self, pos):
        second = pos // self.side
        return (pos % self.side + self.side - second) % self.side, second

    def peers(self):
        peers = [self.device((self.first + d) % self.side, self.second) for d in range(1, self.side)]
        peers += [self.device(self.first, (self.second + d) % self.side) for d in range(1, self.side)]
        return [*peers, self.partner()]

    def greet(self):
        for peer in self.peers():
            pl.semaphore_signal(pltpu.get_barrier_semaphore(), inc=1, device_id=peer, device_id_type=MESH)

    def meet(self):
        pl.semaphore_wait(pltpu.get_barrier_semaphore(), 2 * self.side - 1)


def far_first(side):
    return sorted(range(1, side), key=lambda d: -min(d, side - d))


def remote(src, dst, send_sem, recv_sem, device):
    return pltpu.make_async_remote_copy(src_ref=src, dst_ref=dst, send_sem=send_sem, recv_sem=recv_sem, device_id=device, device_id_type=MESH)


def norm_rows(r_ref, gain, shift, buf, tile):
    rows = pl.ds(pl.multiple_of(tile * TILE, TILE), TILE)
    v = r_ref[rows, :].astype(F32)
    mean = jnp.mean(v, axis=-1, keepdims=True)
    v = v - mean
    var = jnp.mean(v * v, axis=-1, keepdims=True)
    buf[0, rows, :] = (v * lax.rsqrt(var + LN_EPS) * gain + shift).astype(BF16)


class Gather:
    def __init__(self, place, buf, send, recv):
        self.place, self.buf, self.send, self.recv = place, buf, send, recv
        self.half = buf.shape[1] // 2
        self.subs = self.half // TILE
        n = place.chips
        self.next = [place.device(*place.at_pos((place.pos + 1) % n)), place.device(*place.at_pos((place.pos + n - 1) % n))]

    def hop(self, dr, s, k):
        rows = pl.ds(dr * self.half + k * TILE, TILE)
        return remote(self.buf.at[s, rows], self.buf.at[s + 1, rows], self.send.at[dr, s, k], self.recv.at[dr, s, k], self.next[dr])

    def start(self, norm, before, meanwhile):
        norm(0)
        norm(self.subs)
        self.place.meet()
        before()

        def step(k, carry):
            norm(k)
            norm(self.subs + k)
            for dr in range(2):
                self.hop(dr, 0, k - 1).start()
            return carry
        lax.fori_loop(1, self.subs, step, 0)
        meanwhile()
        for dr in range(2):
            self.hop(dr, 0, self.subs - 1).start()

    def take(self, s, k):
        for dr in range(2):
            self.hop(dr, s - 1, k).wait_recv()

            @pl.when(s < self.place.chips - 1)
            def _():
                self.hop(dr, s, k).start()

    def sent(self, s):
        @pl.when(s < self.place.chips - 1)
        def _():
            for dr in range(2):
                for k in range(self.subs):
                    self.hop(dr, s, k).wait_send()

    def run(self, part):
        n = self.place.chips // 2
        for k in range(self.subs):
            self.take(1, k)

        def step(j, carry):
            for h in range(2):
                for k in range(self.subs):
                    @pl.when(j < n)
                    def _():
                        self.take(2 * j + h, k)
                    part(j - 1, h * self.subs + k)
            return carry
        lax.fori_loop(1, n + 1, step, 0)


class Scatter:
    def __init__(self, place, buf, r1, sums, mid, r2, s1_send, s1_recv, mid_send, mid_recv, s2_send, s2_recv):
        self.place, self.buf, self.r1, self.sums, self.mid, self.r2 = place, buf, r1, sums, mid, r2
        self.mid_send, self.mid_recv = mid_send, mid_recv
        self.s1_send, self.s1_recv, self.s2_send, self.s2_recv = s1_send, s1_recv, s2_send, s2_recv
        self.half = buf.shape[1] // 2

    def rows(self, dr):
        return pl.ds(dr * self.half, self.half)

    def first_copy(self, slot, dr, j, first, second):
        p = self.place
        return remote(self.buf.at[slot, self.rows(dr)], self.r1.at[j, second, self.rows(dr)], self.s1_send.at[j, second, dr],
                      self.s1_recv.at[j, second, dr], p.device(first, p.second))

    def send_slot(self, slot):
        p = self.place
        for dr in range(2):
            pos = (p.pos + (p.chips - slot if dr == 0 else slot)) % p.chips
            first, second = p.at_pos(pos)
            away = (first + p.side - p.first) % p.side

            @pl.when(away != 0)
            def _():
                self.first_copy(slot, dr, p.side - 1 - away, first, second).start()

    def slot_of(self, first, second, dr):
        p = self.place
        pos = p.pos_of(first, second)
        return (p.pos + p.chips - pos) % p.chips if dr == 0 else (pos + p.chips - p.pos) % p.chips

    def arrived(self, second, dr):
        for j in range(self.place.side - 1):
            self.first_copy(0, dr, j, self.place.first, second).wait_recv()

    def total(self, second, dr, rows):
        v = self.buf[self.slot_of(self.place.first, second, dr), rows, :].astype(F32)
        for j in range(self.place.side - 1):
            v = v + self.r1[j, second, rows, :].astype(F32)
        return v

    def tile(self, dr, k):
        return pl.ds(pl.multiple_of(dr * self.half + k * TILE, TILE), TILE)

    def mid_copy(self, dr, k):
        p = self.place
        step = 1 if dr == 0 else p.side - 1
        rows = self.tile(dr, k)
        return remote(self.sums.at[1, rows], self.mid.at[rows], self.mid_send.at[dr, k], self.mid_recv.at[dr, k],
                      p.device(p.first, (p.second + step) % p.side))

    def end_copy(self, d, dr, k):
        p = self.place
        at = 0 if d == 1 else 1
        rows = self.tile(dr, k)
        return remote(self.sums.at[d - 1, rows], self.r2.at[at, rows], self.s2_send.at[at, dr, k], self.s2_recv.at[at, dr, k],
                      p.device(p.first, (p.second + d) % p.side))

    def add(self, d, dr, k, with_mid):
        second = (self.place.second + d) % self.place.side
        rows = self.tile(dr, k)
        v = self.total(second, dr, rows)
        if with_mid:
            self.mid_copy(dr, k).wait_recv()
            v = v + self.mid[rows, :]
        self.sums[d - 1, rows, :] = v

    def tiles(self, fn):
        def one(k, carry):
            fn(k)
            return carry
        lax.fori_loop(0, self.half // TILE, one, 0)

    def finish(self, r_ref, bias, out_ref):
        p = self.place

        def pieces(group, with_mid, copy):
            for d, dr in group:
                self.arrived((p.second + d) % p.side, dr)

            def one(k):
                for d, dr in group:
                    self.add(d, dr, k, with_mid)
                    copy(d, dr, k).start()
            self.tiles(one)

        ends = [(1, 1), (p.side - 1, 0)] if p.side > 2 else [(1, 0), (1, 1)]
        pieces(ends, False, self.end_copy)
        if p.side > 2:
            pieces([(2, 0), (2, 1)], False, lambda d, dr, k: self.mid_copy(dr, k))
            more = [(1, 0), (p.side - 1, 1)]
            pieces(more, True, self.end_copy)
            ends = ends + more
        for dr in range(2):
            self.arrived(p.second, dr)

        def last(k):
            for dr in range(2):
                rows = self.tile(dr, k)
                for d, half in ends:
                    if half == dr:
                        self.end_copy(d, dr, k).wait_recv()
                v = self.total(p.second, dr, rows)
                for j in range(self.r2.shape[0]):
                    v = v + self.r2[j, rows, :]
                out_ref[rows, :] = (r_ref[rows, :] + v + bias).astype(out_ref.dtype)
        self.tiles(last)

        def sent(k):
            if p.side > 2:
                for dr in range(2):
                    self.mid_copy(dr, k).wait_send()
            for d, dr in ends:
                self.end_copy(d, dr, k).wait_send()
        self.tiles(sent)
        for dr in range(2):
            for j in range(p.side - 1):
                for second in range(p.side):
                    self.first_copy(0, dr, j, p.first, second).wait_send()


class Share:
    def __init__(self, place, pairs, local, send, recv):
        self.place, self.pairs, self.local, self.send, self.recv = place, pairs, local, send, recv

    def load(self, i):
        src, own, _ = self.pairs[i]
        return pltpu.make_async_copy(src, own, self.local.at[i])

    def give(self, i):
        _, own, other = self.pairs[i]
        return remote(own, other, self.send.at[i], self.recv.at[i], self.place.partner())


def attn_kernel(group_size, layer, n_seq, r_ref, norm_ref, bias_ref, wqkv_ref, wout_ref, out_ref,
                buf, w, wo, qkv, kvp, att, atts, w4, psum, r1, sums, r2, wl, ws, wr, ag_send, ag_recv, kv_send, kv_recv,
                at_send, at_recv, f_send, f_recv, w4_send, w4_recv, s1_send, s1_recv, s2_send, s2_recv):
    place = Place(group_size)
    side, n_chunks, hd = place.side, att.shape[0], att.shape[3] // 2
    slots, block, model = buf.shape
    per_seq = block // n_seq
    per_chunk = block // n_chunks
    width = model // side
    share = Share(place, [(wout_ref.at[layer], wo.at[pl.ds(0, hd)], wo.at[pl.ds(hd, hd)])]
                  + [(wqkv_ref.at[layer, t], w.at[:, pl.ds(t * hd, hd)], w.at[:, pl.ds((3 + t) * hd, hd)]) for t in range(3)], wl, ws, wr)
    place.greet()
    for i in range(4):
        share.load(i).start()
    gather = Gather(place, buf, ag_send, ag_recv)

    def norm(tile):
        norm_rows(r_ref, norm_ref[layer, 0:1, :], norm_ref[layer, 1:2, :], buf, tile)

    def col(first):
        return pl.ds(pl.multiple_of(first * width, width), width)

    def w_copy(d, h):
        first = (place.first + d) % side
        rows = pl.ds(h * hd, hd)
        return remote(wo.at[rows, col(first)], w4.at[side - 1 - d, rows], w4_send.at[side - 1 - d, h], w4_recv.at[side - 1 - d, h],
                      place.device(first, place.second))

    def share_out():
        share.load(0).wait()
        share.give(0).start()
        for d in far_first(side):
            w_copy(d, 0).start()

    def share_qkv():
        for i in range(1, 4):
            share.load(i).wait()
            share.give(i).start()
    gather.start(norm, share_out, share_qkv)
    share.give(0).wait_recv()
    for d in far_first(side):
        w_copy(d, 1).start()

    def kv_copy(j, h):
        pair = pl.ds(2 * j, 2)
        return remote(qkv.at[pair, :, pl.ds(3 * hd * h + hd, 2 * hd)], kvp.at[pair, :, pl.ds(2 * hd * (1 - h), 2 * hd)],
                      kv_send.at[j, h], kv_recv.at[j, h], place.partner())

    wide = 2 * hd

    def part(j, i):
        if i % 2 == 0:
            if i == 0:
                @pl.when(j == 0)
                def _():
                    for t in range(3):
                        share.give(1 + t).wait_recv()
            cols = pl.ds(i // 2 * wide, wide)
            rows = buf[pl.ds(2 * j, 2)].reshape(2 * block, model)
            qkv[pl.ds(2 * j, 2), :, cols] = jnp.dot(rows, w[:, cols], preferred_element_type=F32).astype(BF16).reshape(2, block, wide)
        if i == 5:
            for h in range(2):
                kv_copy(j, h).start()
            gather.sent(2 * j)
            gather.sent(2 * j + 1)
    gather.run(part)

    for j in range(slots // 2):
        for h in range(2):
            kv_copy(j, h).wait_recv()

    nq, nk = slots * per_chunk, slots * per_seq

    def rows_of(chunk):
        return pl.ds(pl.multiple_of(chunk * per_chunk, per_chunk), per_chunk)

    def attend(chunk):
        seq = chunk * per_chunk // per_seq
        lower = chunk * per_chunk // (block // 2)
        keys = pl.ds(pl.multiple_of(seq * per_seq, per_seq), per_seq)

        def head_of(h, carry):
            def cols(base, k):
                return pl.ds(pl.multiple_of(h * base + k * hd, hd), hd)
            q = qkv[:, rows_of(chunk), cols(3 * hd, 0)].reshape(nq, hd)
            k0 = qkv[:, keys, cols(3 * hd, 1)].reshape(nk, hd)
            v0 = qkv[:, keys, cols(3 * hd, 2)].reshape(nk, hd)
            k1 = kvp[:, keys, cols(2 * hd, 0)].reshape(nk, hd)
            v1 = kvp[:, keys, cols(2 * hd, 1)].reshape(nk, hd)
            dims = (((1,), (1,)), ((), ()))
            s0 = lax.dot_general(q, k0, dims, preferred_element_type=F32) * hd ** -0.5
            s1 = lax.dot_general(q, k1, dims, preferred_element_type=F32) * hd ** -0.5
            top = jnp.maximum(jnp.max(s0, axis=-1, keepdims=True), jnp.max(s1, axis=-1, keepdims=True))
            e0 = jnp.exp(s0 - top)
            e1 = jnp.exp(s1 - top)
            inv = 1.0 / (jnp.sum(e0, axis=-1, keepdims=True) + jnp.sum(e1, axis=-1, keepdims=True))
            a = jnp.dot((e0 * inv).astype(BF16), v0, preferred_element_type=F32)
            a = (a + jnp.dot((e1 * inv).astype(BF16), v1, preferred_element_type=F32)).astype(BF16)
            for slot in range(slots):
                pos = (place.pos + (slots - slot) * (1 - lower) + slot * lower) % slots
                att[chunk, pos, :, cols(hd, 0)] = a[slot * per_chunk:(slot + 1) * per_chunk]
            return carry
        lax.fori_loop(0, 2, head_of, 0)
        for d in near:
            a_copy(chunk, d).start()

    near = [d for d in range(1, side) if min(d, side - d) == 1]

    def f_copy(seq, h):
        cols = pl.ds(h * hd, hd)
        return remote(atts.at[side - 2 if h == 0 else 0, seq, :, :, cols], atts.at[1, seq, :, :, cols], f_send.at[seq, h], f_recv.at[seq, h],
                      place.device((place.first + (1 if h == 0 else side - 1)) % side, place.second))

    def forward(seq):
        for d in near:
            a_copy(seq, d).wait_recv()
        if side > 2:
            for h in range(2):
                f_copy(seq, h).start()

    def a_copy(seq, d):
        return remote(att.at[seq], atts.at[side - 1 - d, seq], at_send.at[seq, side - 1 - d], at_recv.at[seq, side - 1 - d],
                      place.device((place.first + d) % side, place.second))

    def p_copy(seq, d):
        second = (place.second + d) % side
        return remote(psum.at[seq, pl.ds(pl.multiple_of(second * side, side), side)], r1.at[side - 1 - d, seq], s1_send.at[seq, side - 1 - d],
                      s1_recv.at[seq, side - 1 - d], place.device(place.first, second))

    def project(seq):
        @pl.when(seq == 0)
        def _():
            for d in range(1, side):
                for h in range(2):
                    w_copy(d, h).wait_recv()
        if side > 2:
            for h in range(2):
                f_copy(seq, h).wait_recv()
        half = width // 2
        for c in range(2):
            own = pl.ds(pl.multiple_of(place.first * width + c * half, half), half)
            cols = pl.ds(c * half, half)
            v = jnp.dot(att[seq].reshape(slots * per_chunk, 2 * hd), wo[:, own], preferred_element_type=F32)
            for j in range(side - 1):
                v = v + jnp.dot(atts[j, seq].reshape(slots * per_chunk, 2 * hd), w4[j, :, cols], preferred_element_type=F32)
            psum[seq, :, :, cols] = v.astype(BF16).reshape(slots, per_chunk, half)
        for d in far_first(side):
            p_copy(seq, d).start()

    def s_copy(seq, d):
        first = (place.first + d) % side
        return remote(sums.at[seq, (first + place.second) % side], r2.at[side - 1 - d, seq], s2_send.at[seq, side - 1 - d],
                      s2_recv.at[seq, side - 1 - d], place.device(first, place.second))

    def add(seq):
        for d in range(1, side):
            p_copy(seq, d).wait_recv()

        def one(i, carry):
            v = psum[seq, place.second * side + i].astype(F32)
            for j in range(side - 1):
                v = v + r1[j, seq, i].astype(F32)
            sums[seq, i] = v
            return carry
        lax.fori_loop(0, side, one, 0)
        for d in far_first(side):
            s_copy(seq, d).start()

    def output(seq):
        rows = rows_of(seq)

        def put(first, v):
            out_ref[rows, col(first)] = r_ref[rows, col(first)].astype(F32) + v + bias_ref[pl.ds(layer, 1), col(first)]
        put(place.first, sums[seq, (place.first + place.second) % side])
        for j in range(side - 1):
            s_copy(seq, side - 1 - j).wait_recv()
            put((place.first + 1 + j) % side, r2[j, seq])

    lag = n_chunks // 2
    stages = ((attend, 0), (forward, lag - 1), (project, lag), (add, lag + 1), (output, lag + 2))

    def step(i, carry):
        for stage, at in stages:
            @pl.when((i >= at) & (i < at + n_chunks))
            def _():
                stage(i - at)
        return carry
    lax.fori_loop(0, n_chunks + lag + 2, step, 0)
    for i in range(4):
        share.give(i).wait_send()
    for j in range(slots // 2):
        for h in range(2):
            kv_copy(j, h).wait_send()
    for d in range(1, side):
        for h in range(2):
            w_copy(d, h).wait_send()
        for seq in range(n_chunks):
            if d in near:
                a_copy(seq, d).wait_send()
            elif d == 2:
                for h in range(2):
                    f_copy(seq, h).wait_send()
            p_copy(seq, d).wait_send()
            s_copy(seq, d).wait_send()


def mlp_kernel(group_size, layer, r_ref, norm_ref, bias_ref, bup_ref, wup_ref, wdown_ref, out_ref,
               buf, wu, wd, bu, u, r1, sums, mid, r2, wl, ws, wr, ag_send, ag_recv, s1_send, s1_recv, mid_send, mid_recv, s2_send, s2_recv):
    place = Place(group_size)
    slots, block, model = buf.shape
    ff = wup_ref.shape[2]
    share = Share(place, [(bup_ref.at[pl.ds(layer, 1)], bu.at[:, pl.ds(0, ff)], bu.at[:, pl.ds(ff, ff)]),
                          (wup_ref.at[layer], wu.at[:, pl.ds(0, ff)], wu.at[:, pl.ds(ff, ff)]),
                          (wdown_ref.at[layer], wd.at[pl.ds(0, ff)], wd.at[pl.ds(ff, ff)])], wl, ws, wr)
    place.greet()
    for i in range(3):
        share.load(i).start()
    gather = Gather(place, buf, ag_send, ag_recv)

    def norm(tile):
        norm_rows(r_ref, norm_ref[layer, 2:3, :], norm_ref[layer, 3:4, :], buf, tile)

    def share_all():
        for i in range(3):
            share.load(i).wait()
            share.give(i).start()
    gather.start(norm, lambda: None, share_all)
    scatter = Scatter(place, buf, r1, sums, mid, r2, s1_send, s1_recv, mid_send, mid_recv, s2_send, s2_recv)
    up_w, down_w = ff // 2, model // 4
    def up(j, c):
        rows = buf[pl.ds(2 * j, 2)].reshape(2 * block, model)
        cols = pl.ds(c * up_w, up_w)
        hidden = jnp.dot(rows, wu[:, cols], preferred_element_type=F32) + bu[:, cols]
        u[:, cols] = jax.nn.gelu(hidden, approximate=True).astype(BF16)

    def down(j, c):
        cols = pl.ds(c * down_w, down_w)
        buf[pl.ds(2 * j, 2), :, cols] = jnp.dot(u[...], wd[:, cols], preferred_element_type=F32).astype(BF16).reshape(2, block, down_w)

    def send_slots(begin, end):
        def one(slot, carry):
            scatter.send_slot(slot)
            return carry
        lax.fori_loop(begin, end, one, 0)

    def part(j, i):
        if i == 0:
            @pl.when(j == 0)
            def _():
                share.give(0).wait_recv()
                share.give(1).wait_recv()

            @pl.when(j == slots // 2 - 1)
            def _():
                send_slots(0, slots - 2)
            up(j, 0)
            up(j, 1)
        elif i == 1:
            up(j, 2)
        elif i == 2:
            up(j, 3)
        elif i == 3:
            @pl.when(j == 0)
            def _():
                share.give(2).wait_recv()
            gather.sent(2 * j)
            gather.sent(2 * j + 1)
            down(j, 0)
        elif i == 4:
            down(j, 1)
        else:
            down(j, 2)
            down(j, 3)
    gather.run(part)
    send_slots(slots - 2, slots)
    scatter.finish(r_ref, bias_ref[pl.ds(layer, 1), :], out_ref)
    for i in range(3):
        share.give(i).wait_send()


def solution(mesh):
    group_size = mesh.shape["tp"]
    side = math.isqrt(group_size // 2)
    chips = side * side
    dma = pltpu.SemaphoreType.DMA
    vmem = pl.BlockSpec(memory_space=pltpu.VMEM)
    hbm = pl.BlockSpec(memory_space=pl.ANY)

    def local_layers(hidden_in, norms, w_qkv, w_out, b_out, w_up, b_up, w_down, b_down):
        n_seq, per_seq, model = hidden_in.shape
        n_layers, head_dim, ff = w_qkv.shape[0], w_qkv.shape[-1], w_up.shape[-1]
        block = n_seq * per_seq
        subs = block // 2 // TILE
        n_chunks = block // TILE
        residual = hidden_in.reshape(block, model)
        w_qkv = w_qkv.transpose(0, 2, 3, 1, 4).reshape(n_layers, 3, model, head_dim)
        w_out = w_out.reshape(n_layers, head_dim, model)
        width = model // side
        ring = [dma((2, chips - 1, subs))] * 2
        rows = pltpu.VMEM((chips, block, model), BF16)

        def params(collective_id):
            return pltpu.CompilerParams(collective_id=collective_id, has_side_effects=True, vmem_limit_bytes=VMEM_LIMIT)

        for layer in range(n_layers):
            residual = pl.pallas_call(
                functools.partial(attn_kernel, group_size, layer, n_seq), name=f"attn{layer}",
                out_shape=jax.ShapeDtypeStruct((block, model), F32),
                in_specs=[vmem, vmem, vmem, hbm, hbm], out_specs=vmem,
                scratch_shapes=[rows, pltpu.VMEM((model, 6 * head_dim), BF16), pltpu.VMEM((2 * head_dim, model), BF16),
                                pltpu.VMEM((chips, block, 6 * head_dim), BF16), pltpu.VMEM((chips, block, 4 * head_dim), BF16),
                                pltpu.VMEM((n_chunks, chips, TILE, 2 * head_dim), BF16),
                                pltpu.VMEM((side - 1, n_chunks, chips, TILE, 2 * head_dim), BF16),
                                pltpu.VMEM((side - 1, 2 * head_dim, width), BF16),
                                pltpu.VMEM((n_chunks, chips, TILE, width), BF16),
                                pltpu.VMEM((side - 1, n_chunks, side, TILE, width), BF16),
                                pltpu.VMEM((n_chunks, side, TILE, width), F32),
                                pltpu.VMEM((side - 1, n_chunks, TILE, width), F32),
                                dma((4,)), dma((4,)), dma((4,)), *ring, dma((chips // 2, 2)), dma((chips // 2, 2)),
                                *[dma((n_chunks, side - 1))] * 2, *[dma((n_chunks, 2))] * 2, *[dma((side - 1, 2))] * 2,
                                *[dma((n_chunks, side - 1))] * 4],
                compiler_params=params(2 * layer),
            )(residual, norms, b_out, w_qkv, w_out)
            residual = pl.pallas_call(
                functools.partial(mlp_kernel, group_size, layer), name=f"mlp{layer}",
                out_shape=jax.ShapeDtypeStruct((block, model), F32 if layer < n_layers - 1 else BF16),
                in_specs=[vmem, vmem, vmem, hbm, hbm, hbm], out_specs=vmem,
                scratch_shapes=[rows, pltpu.VMEM((model, 2 * ff), BF16), pltpu.VMEM((2 * ff, model), BF16), pltpu.VMEM((1, 2 * ff), F32),
                                pltpu.VMEM((2 * block, 2 * ff), BF16), pltpu.VMEM((side - 1, side, block, model), BF16),
                                pltpu.VMEM((side - 1, block, model), F32), pltpu.VMEM((block, model), F32),
                                pltpu.VMEM((min(2, side - 1), block, model), F32), dma((3,)), dma((3,)), dma((3,)), *ring,
                                *[dma((side - 1, side, 2))] * 2, *[dma((2, subs))] * 2, *[dma((2, 2, subs))] * 2],
                compiler_params=params(2 * layer + 1),
            )(residual, norms, b_down, b_up, w_up, w_down)
        return residual.reshape(n_seq, per_seq, model)

    in_specs = (P('dp', 'tp', None), P(), P(None, None, None, 'tp', None), P(None, 'tp', None, None), P(), P(None, None, 'tp'), P(None, 'tp'), P(None, 'tp', None), P())
    return jax.shard_map(local_layers, mesh=mesh, in_specs=in_specs, out_specs=P('dp', 'tp', None), check_vma=False)
```

time: 858 us -> 654 us (0.76)
  Pallas kernels: 834 us -> 651 us
  local copies, waits for them, and re-layouts: 22.1 us -> 2.06 us
    pallas_call x2, Pallas kernels: 405 us -> 285 us  [local_layers(): pl.pallas_call(functools.partial(attn_kernel, group_size, layer, n_seq),...]
    pallas_call x2, Pallas kernels: 428 us -> 367 us  [local_layers(): pl.pallas_call(functools.partial(mlp_kernel, group_size, layer), name=f'm...]
    reshape x1 -> x0, local copies, waits for them, and re-layouts: 8.69 us -> none  [local_layers(): w_qkv = w_qkv.reshape(n_layers, model, 3 * head_dim)]
    unnamed x8 -> x1, local copies, waits for them, and re-layouts: 10.7 us -> 2.06 us
where the time goes in v2:
time: 654 us; the launch traced here: 653 us
  Pallas kernels  651 us (100%)
    pallas_call x2, Pallas kernels, local_layers(): pl.pallas_call(functools.partial(mlp_kernel, group_size, layer), name=f'm...  367 us
    pallas_call x2, Pallas kernels, local_layers(): pl.pallas_call(functools.partial(attn_kernel, group_size, layer, n_seq),...  285 us

profile of v2, /device:TPU:96, one launch (start us, length us, event | category | flops | bytes accessed | tf_op | source)
XLA Modules:
  0.0 653.3 jit_solution(8502539954857095143)
XLA Ops:
  0.0 143.4 %attn0.1.r_ref = f32[96,4096]{1,0:T(8,128)} custom-call(bf16[96,4096]{1,0:T(8,128)(2,1)} %bitcast.13, f32[2,4,4096]{2,1,0:T(4,128)} %norm_ref.7, f32[2,4096]{1,0:T(2,128)} %bias_ref.6, bf16[2,3,4096,128]{3,2,1,0:T(8,128)(2,1)} %bitcast.8, bf16[2,128,4096]{2,1,0:T(8,128)(2,1)} %bitcast.10), custom_call_target="tpu_custom_call" | custom-call | tf_op jit(solution)/shard_map/attn0/pallas_call | solution.py:577
  143.4 183.6 %mlp0.1.r_ref = f32[96,4096]{1,0:T(8,128)} custom-call(f32[96,4096]{1,0:T(8,128)} %attn0.1.r_ref, f32[2,4,4096]{2,1,0:T(4,128)} %norm_ref.7, f32[2,4096]{1,0:T(2,128)} %bias_ref.7, f32[2,512]{1,0:T(2,128)} %bup_ref.3, bf16[2,4096,512]{2,1,0:T(8,128)(2,1)} %wup_ref.3, bf16[2,512,4096]{2,1,0:T(8,128)(2,1)} %wdown_ref.3), custom_call_target="tpu_custom_call" | custom-call | tf_op jit(solution)/shard_map/mlp0/pallas_call | solution.py:595
  327.0 141.3 %attn1.1.r_ref = f32[96,4096]{1,0:T(8,128)} custom-call(f32[96,4096]{1,0:T(8,128)} %mlp0.1.r_ref, f32[2,4,4096]{2,1,0:T(4,128)} %norm_ref.7, f32[2,4096]{1,0:T(2,128)} %bias_ref.6, bf16[2,3,4096,128]{3,2,1,0:T(8,128)(2,1)} %bitcast.9, bf16[2,128,4096]{2,1,0:T(8,128)(2,1)} %bitcast.11), custom_call_target="tpu_custom_call" | custom-call | tf_op jit(solution)/shard_map/attn1/pallas_call | solution.py:577
  468.3 182.9 %mlp1.1 = bf16[96,4096]{1,0:T(8,128)(2,1)} custom-call(f32[96,4096]{1,0:T(8,128)} %attn1.1.r_ref, f32[2,4,4096]{2,1,0:T(4,128)} %norm_ref.7, f32[2,4096]{1,0:T(2,128)} %bias_ref.7, f32[2,512]{1,0:T(2,128)} %bup_ref.3, bf16[2,4096,512]{2,1,0:T(8,128)(2,1)} %wup_ref.3, bf16[2,512,4096]{2,1,0:T(8,128)(2,1)} %wdown_ref.3), custom_call_target="tpu_custom_call" | custom-call | tf_op jit(solution)/shard_map/mlp1/pallas_call | solution.py:595
  651.3 2.1 copy.12

commit v3 on v2

--- a/solution.py
+++ b/solution.py
@@ -81,11 +81,12 @@
         self.half = buf.shape[1] // 2
         self.subs = self.half // TILE
         n = place.chips
-        self.next = [place.device(*place.at_pos((place.pos + 1) % n)), place.device(*place.at_pos((place.pos + n - 1) % n))]
+        self.next = [place.device(*place.at_pos((place.pos + d) % n))["tp"] for d in (1, n - 1)]
 
     def hop(self, dr, s, k):
-        rows = pl.ds(dr * self.half + k * TILE, TILE)
-        return remote(self.buf.at[s, rows], self.buf.at[s + 1, rows], self.send.at[dr, s, k], self.recv.at[dr, s, k], self.next[dr])
+        rows = pl.ds(pl.multiple_of(dr * self.half + k * TILE, TILE), TILE)
+        return remote(self.buf.at[s, rows], self.buf.at[s + 1, rows], self.send.at[dr, s, k], self.recv.at[dr, s, k],
+                      {"tp": self.next[0] * (1 - dr) + self.next[1] * dr})
 
     def start(self, norm, before, meanwhile):
         norm(0)
@@ -150,14 +151,14 @@
         return remote(self.buf.at[slot, self.rows(dr)], self.r1.at[j, second, self.rows(dr)], self.s1_send.at[j, second, dr],
                       self.s1_recv.at[j, second, dr], p.device(first, p.second))
 
-    def send_slot(self, slot):
+    def send_rows(self, d, dr, begin, end):
         p = self.place
-        for dr in range(2):
-            pos = (p.pos + (p.chips - slot if dr == 0 else slot)) % p.chips
-            first, second = p.at_pos(pos)
-            away = (first + p.side - p.first) % p.side
-
-            @pl.when(away != 0)
+        second = (p.second + d) % p.side
+        for away in far_first(p.side):
+            first = (p.first + away) % p.side
+            slot = self.slot_of(first, second, dr)
+
+            @pl.when((slot >= begin) & (slot < end))
             def _():
                 self.first_copy(slot, dr, p.side - 1 - away, first, second).start()
 
@@ -208,7 +209,7 @@
             return carry
         lax.fori_loop(0, self.half // TILE, one, 0)
 
-    def finish(self, r_ref, bias, out_ref):
+    def finish(self, res, bias, out_ref):
         p = self.place
 
         def pieces(group, with_mid, copy):
@@ -240,7 +241,7 @@
                 v = self.total(p.second, dr, rows)
                 for j in range(self.r2.shape[0]):
                     v = v + self.r2[j, rows, :]
-                out_ref[rows, :] = (r_ref[rows, :] + v + bias).astype(out_ref.dtype)
+                out_ref[rows, :] = (res[rows, :] + v + bias).astype(out_ref.dtype)
         self.tiles(last)
 
         def sent(k):
@@ -269,17 +270,38 @@
         return remote(own, other, self.send.at[i], self.recv.at[i], self.place.partner())
 
 
-def attn_kernel(group_size, layer, n_seq, r_ref, norm_ref, bias_ref, wqkv_ref, wout_ref, out_ref,
-                buf, w, wo, qkv, kvp, att, atts, w4, psum, r1, sums, r2, wl, ws, wr, ag_send, ag_recv, kv_send, kv_recv,
-                at_send, at_recv, f_send, f_recv, w4_send, w4_recv, s1_send, s1_recv, s2_send, s2_recv):
+def layer_kernel(group_size, layer, n_seq, r_ref, norm_ref, bout_ref, bdown_ref, bup_ref, wqkv_ref, wout_ref, wup_ref, wdown_ref, out_ref,
+                 buf, wu, wd, bu, u, r1, sums, mid, r2, qkv, kvp, w4, res,
+                 wl, ws, wr, free, ag_send, ag_recv, ag2_send, ag2_recv, kv_send, kv_recv, a_send, a_recv, f_send, f_recv, w4_send, w4_recv,
+                 p_send, p_recv, s_send, s_recv, s1_send, s1_recv, mid_send, mid_recv, s2_send, s2_recv):
     place = Place(group_size)
-    side, n_chunks, hd = place.side, att.shape[0], att.shape[3] // 2
     slots, block, model = buf.shape
-    per_seq = block // n_seq
-    per_chunk = block // n_chunks
-    width = model // side
-    share = Share(place, [(wout_ref.at[layer], wo.at[pl.ds(0, hd)], wo.at[pl.ds(hd, hd)])]
-                  + [(wqkv_ref.at[layer, t], w.at[:, pl.ds(t * hd, hd)], w.at[:, pl.ds((3 + t) * hd, hd)]) for t in range(3)], wl, ws, wr)
+    side, hd, ff = place.side, w4.shape[1] // 2, wup_ref.shape[2]
+    n_chunks, per_seq, width = block // TILE, block // n_seq, model // place.side
+    per_row = side
+    every = slots * TILE
+    share = Share(place, [(wout_ref.at[layer], wd.at[pl.ds(0, hd)], wd.at[pl.ds(hd, hd)])]
+                  + [(wqkv_ref.at[layer, t], wu.at[:, pl.ds(t * hd, hd)], wu.at[:, pl.ds((3 + t) * hd, hd)]) for t in range(3)]
+                  + [(bup_ref.at[pl.ds(layer, 1)], bu.at[:, pl.ds(0, ff)], bu.at[:, pl.ds(ff, ff)]),
+                     (wup_ref.at[layer], wu.at[:, pl.ds(0, ff)], wu.at[:, pl.ds(ff, ff)]),
+                     (wdown_ref.at[layer], wd.at[pl.ds(0, ff)], wd.at[pl.ds(ff, ff)])], wl, ws, wr)
+    area = [2 * hd + i * every for i in range(3)]
+
+    def piece(i, n):
+        return wd.at[pl.ds(area[i], every), pl.ds(pl.multiple_of(n * 2 * hd, 2 * hd), 2 * hd)]
+
+    def heads(j, chunk):
+        return (piece(2, chunk), piece(2, n_chunks + chunk), piece(1, n_chunks + chunk), piece(1, chunk))[j]
+
+    def partial(chunk):
+        over = chunk // per_row
+        row = pl.multiple_of(area[0] + every * over * (chunk - per_row + 1), TILE)
+        col = pl.multiple_of(width * (chunk * (1 - over) + (per_row - 1) * over), width)
+        return row, pl.ds(col, width)
+
+    def cell(chunk):
+        return chunk // per_row, pl.ds(pl.multiple_of(chunk % per_row * width, width), width)
+
     place.greet()
     for i in range(4):
         share.load(i).start()
@@ -294,7 +316,7 @@
     def w_copy(d, h):
         first = (place.first + d) % side
         rows = pl.ds(h * hd, hd)
-        return remote(wo.at[rows, col(first)], w4.at[side - 1 - d, rows], w4_send.at[side - 1 - d, h], w4_recv.at[side - 1 - d, h],
+        return remote(wd.at[rows, col(first)], w4.at[side - 1 - d, rows], w4_send.at[side - 1 - d, h], w4_recv.at[side - 1 - d, h],
                       place.device(first, place.second))
 
     def share_out():
@@ -317,43 +339,44 @@
         return remote(qkv.at[pair, :, pl.ds(3 * hd * h + hd, 2 * hd)], kvp.at[pair, :, pl.ds(2 * hd * (1 - h), 2 * hd)],
                       kv_send.at[j, h], kv_recv.at[j, h], place.partner())
 
-    wide = 2 * hd
-
-    def part(j, i):
+    def qkv_part(j, i):
         if i % 2 == 0:
             if i == 0:
                 @pl.when(j == 0)
                 def _():
                     for t in range(3):
                         share.give(1 + t).wait_recv()
-            cols = pl.ds(i // 2 * wide, wide)
+            cols = pl.ds(i // 2 * 2 * hd, 2 * hd)
             rows = buf[pl.ds(2 * j, 2)].reshape(2 * block, model)
-            qkv[pl.ds(2 * j, 2), :, cols] = jnp.dot(rows, w[:, cols], preferred_element_type=F32).astype(BF16).reshape(2, block, wide)
+            qkv[pl.ds(2 * j, 2), :, cols] = jnp.dot(rows, wu[:, cols], preferred_element_type=F32).astype(BF16).reshape(2, block, 2 * hd)
         if i == 5:
             for h in range(2):
                 kv_copy(j, h).start()
             gather.sent(2 * j)
             gather.sent(2 * j + 1)
-    gather.run(part)
-
+    gather.run(qkv_part)
     for j in range(slots // 2):
         for h in range(2):
             kv_copy(j, h).wait_recv()
-
-    nq, nk = slots * per_chunk, slots * per_seq
+    for i in range(1, 4):
+        share.give(i).wait_send()
+    for i in (4, 5):
+        share.load(i).start()
+
+    nk = slots * per_seq
 
     def rows_of(chunk):
-        return pl.ds(pl.multiple_of(chunk * per_chunk, per_chunk), per_chunk)
+        return pl.ds(pl.multiple_of(chunk * TILE, TILE), TILE)
 
     def attend(chunk):
-        seq = chunk * per_chunk // per_seq
-        lower = chunk * per_chunk // (block // 2)
+        seq = chunk * TILE // per_seq
+        lower = chunk * TILE // (block // 2)
         keys = pl.ds(pl.multiple_of(seq * per_seq, per_seq), per_seq)
 
         def head_of(h, carry):
             def cols(base, k):
                 return pl.ds(pl.multiple_of(h * base + k * hd, hd), hd)
-            q = qkv[:, rows_of(chunk), cols(3 * hd, 0)].reshape(nq, hd)
+            q = qkv[:, rows_of(chunk), cols(3 * hd, 0)].reshape(every, hd)
             k0 = qkv[:, keys, cols(3 * hd, 1)].reshape(nk, hd)
             v0 = qkv[:, keys, cols(3 * hd, 2)].reshape(nk, hd)
             k1 = kvp[:, keys, cols(2 * hd, 0)].reshape(nk, hd)
@@ -369,83 +392,106 @@
             a = (a + jnp.dot((e1 * inv).astype(BF16), v1, preferred_element_type=F32)).astype(BF16)
             for slot in range(slots):
                 pos = (place.pos + (slots - slot) * (1 - lower) + slot * lower) % slots
-                att[chunk, pos, :, cols(hd, 0)] = a[slot * per_chunk:(slot + 1) * per_chunk]
+                wd[pl.ds(pl.multiple_of(area[1] + pos * TILE, TILE), TILE),
+                   pl.ds(pl.multiple_of(chunk * 2 * hd + h * hd, hd), hd)] = a[slot * TILE:(slot + 1) * TILE]
             return carry
         lax.fori_loop(0, 2, head_of, 0)
         for d in near:
             a_copy(chunk, d).start()
 
-    near = [d for d in range(1, side) if min(d, side - d) == 1]
-
-    def f_copy(seq, h):
+    near = (1, side - 1)
+
+    def a_copy(chunk, d):
+        return remote(heads(side - 1, chunk), heads(side - 1 - d, chunk), a_send.at[chunk, d // 2], a_recv.at[chunk, d // 2],
+                      place.device((place.first + d) % side, place.second))
+
+    def f_copy(chunk, h):
         cols = pl.ds(h * hd, hd)
-        return remote(atts.at[side - 2 if h == 0 else 0, seq, :, :, cols], atts.at[1, seq, :, :, cols], f_send.at[seq, h], f_recv.at[seq, h],
+        return remote(heads(2 - 2 * h, chunk).at[:, cols], heads(1, chunk).at[:, cols], f_send.at[chunk, h], f_recv.at[chunk, h],
                       place.device((place.first + (1 if h == 0 else side - 1)) % side, place.second))
 
-    def forward(seq):
+    def forward(chunk):
         for d in near:
-            a_copy(seq, d).wait_recv()
-        if side > 2:
-            for h in range(2):
-                f_copy(seq, h).start()
-
-    def a_copy(seq, d):
-        return remote(att.at[seq], atts.at[side - 1 - d, seq], at_send.at[seq, side - 1 - d], at_recv.at[seq, side - 1 - d],
-                      place.device((place.first + d) % side, place.second))
-
-    def p_copy(seq, d):
+            a_copy(chunk, d).wait_recv()
+        for h in range(2):
+            f_copy(chunk, h).start()
+
+        @pl.when(chunk == 0)
+        def _():
+            for i in (4, 5):
+                share.load(i).wait()
+                share.give(i).start()
+
+    def p_copy(chunk, d):
         second = (place.second + d) % side
-        return remote(psum.at[seq, pl.ds(pl.multiple_of(second * side, side), side)], r1.at[side - 1 - d, seq], s1_send.at[seq, side - 1 - d],
-                      s1_recv.at[seq, side - 1 - d], place.device(place.first, second))
-
-    def project(seq):
-        @pl.when(seq == 0)
+        row, cols = partial(chunk)
+        at, there = cell(chunk)
+        return remote(wd.at[pl.ds(pl.multiple_of(row + second * side * TILE, TILE), side * TILE), cols],
+                      r1.at[side - 1 - d, at, pl.ds(0, side * TILE), there], p_send.at[chunk, side - 1 - d], p_recv.at[chunk, side - 1 - d],
+                      place.device(place.first, second))
+
+    def project(chunk):
+        @pl.when(chunk == 0)
         def _():
             for d in range(1, side):
                 for h in range(2):
                     w_copy(d, h).wait_recv()
-        if side > 2:
-            for h in range(2):
-                f_copy(seq, h).wait_recv()
+        for h in range(2):
+            f_copy(chunk, h).wait_recv()
         half = width // 2
+        row, cols = partial(chunk)
         for c in range(2):
             own = pl.ds(pl.multiple_of(place.first * width + c * half, half), half)
-            cols = pl.ds(c * half, half)
-            v = jnp.dot(att[seq].reshape(slots * per_chunk, 2 * hd), wo[:, own], preferred_element_type=F32)
+            v = jnp.dot(heads(side - 1, chunk)[...], wd[pl.ds(0, 2 * hd), own], preferred_element_type=F32)
             for j in range(side - 1):
-                v = v + jnp.dot(atts[j, seq].reshape(slots * per_chunk, 2 * hd), w4[j, :, cols], preferred_element_type=F32)
-            psum[seq, :, :, cols] = v.astype(BF16).reshape(slots, per_chunk, half)
+                v = v + jnp.dot(heads(j, chunk)[...], w4[j, :, pl.ds(c * half, half)], preferred_element_type=F32)
+            wd[pl.ds(row, every), pl.ds(pl.multiple_of(cols.start + c * half, half), half)] = v.astype(BF16)
         for d in far_first(side):
-            p_copy(seq, d).start()
-
-    def s_copy(seq, d):
+            p_copy(chunk, d).start()
+
+    def s_copy(chunk, d):
         first = (place.first + d) % side
-        return remote(sums.at[seq, (first + place.second) % side], r2.at[side - 1 - d, seq], s2_send.at[seq, side - 1 - d],
-                      s2_recv.at[seq, side - 1 - d], place.device(first, place.second))
-
-    def add(seq):
+        at, there = cell(chunk)
+        i = (first + place.second) % side
+        return remote(sums.at[at, pl.ds(pl.multiple_of(i * TILE, TILE), TILE), there],
+                      r2.at[0, rows_of(chunk), pl.ds((side - 1 - d) * width, width)], s_send.at[chunk, side - 1 - d], s_recv.at[chunk, side - 1 - d],
+                      place.device(first, place.second))
+
+    def add(chunk):
         for d in range(1, side):
-            p_copy(seq, d).wait_recv()
+            p_copy(chunk, d).wait_recv()
+        row, cols = partial(chunk)
+        at, there = cell(chunk)
 
         def one(i, carry):
-            v = psum[seq, place.second * side + i].astype(F32)
+            rows = rows_of(i)
+            v = wd[pl.ds(pl.multiple_of(row + (place.second * side + i) * TILE, TILE), TILE), cols].astype(F32)
             for j in range(side - 1):
-                v = v + r1[j, seq, i].astype(F32)
-            sums[seq, i] = v
+                v = v + r1[j, at, rows, there].astype(F32)
+            sums[at, rows, there] = v
             return carry
         lax.fori_loop(0, side, one, 0)
         for d in far_first(side):
-            s_copy(seq, d).start()
-
-    def output(seq):
-        rows = rows_of(seq)
+            s_copy(chunk, d).start()
+
+    gather2 = Gather(place, buf, ag2_send, ag2_recv)
+    subs = gather2.subs
+
+    def output(chunk):
+        rows = rows_of(chunk)
+        at, there = cell(chunk)
 
         def put(first, v):
-            out_ref[rows, col(first)] = r_ref[rows, col(first)].astype(F32) + v + bias_ref[pl.ds(layer, 1), col(first)]
-        put(place.first, sums[seq, (place.first + place.second) % side])
+            res[rows, col(first)] = r_ref[rows, col(first)].astype(F32) + v + bout_ref[pl.ds(layer, 1), col(first)]
+        put(place.first, sums[at, pl.ds(pl.multiple_of((place.first + place.second) % side * TILE, TILE), TILE), there])
         for j in range(side - 1):
-            s_copy(seq, side - 1 - j).wait_recv()
-            put((place.first + 1 + j) % side, r2[j, seq])
+            s_copy(chunk, side - 1 - j).wait_recv()
+            put((place.first + 1 + j) % side, r2[0, rows, pl.ds(j * width, width)])
+        norm_rows(res, norm_ref[layer, 2:3, :], norm_ref[layer, 3:4, :], buf, chunk)
+
+        @pl.when(chunk > 0)
+        def _():
+            gather2.hop((chunk - 1) // subs, 0, (chunk - 1) % subs).start()
 
     lag = n_chunks // 2
     stages = ((attend, 0), (forward, lag - 1), (project, lag), (add, lag + 1), (output, lag + 2))
@@ -457,47 +503,31 @@
                 stage(i - at)
         return carry
     lax.fori_loop(0, n_chunks + lag + 2, step, 0)
-    for i in range(4):
-        share.give(i).wait_send()
+
+    def done(chunk, carry):
+        for d in range(1, side):
+            p_copy(chunk, d).wait_send()
+            s_copy(chunk, d).wait_send()
+        for d in near:
+            a_copy(chunk, d).wait_send()
+        for h in range(2):
+            f_copy(chunk, h).wait_send()
+        return carry
+    lax.fori_loop(0, n_chunks, done, 0)
+    gather2.hop(1, 0, subs - 1).start()
+    for d in range(1, side):
+        for h in range(2):
+            w_copy(d, h).wait_send()
+    share.give(0).wait_send()
+    share.load(6).start()
+    pl.semaphore_signal(free, inc=1, device_id=place.partner(), device_id_type=MESH)
     for j in range(slots // 2):
         for h in range(2):
             kv_copy(j, h).wait_send()
-    for d in range(1, side):
-        for h in range(2):
-            w_copy(d, h).wait_send()
-        for seq in range(n_chunks):
-            if d in near:
-                a_copy(seq, d).wait_send()
-            elif d == 2:
-                for h in range(2):
-                    f_copy(seq, h).wait_send()
-            p_copy(seq, d).wait_send()
-            s_copy(seq, d).wait_send()
-
-
-def mlp_kernel(group_size, layer, r_ref, norm_ref, bias_ref, bup_ref, wup_ref, wdown_ref, out_ref,
-               buf, wu, wd, bu, u, r1, sums, mid, r2, wl, ws, wr, ag_send, ag_recv, s1_send, s1_recv, mid_send, mid_recv, s2_send, s2_recv):
-    place = Place(group_size)
-    slots, block, model = buf.shape
-    ff = wup_ref.shape[2]
-    share = Share(place, [(bup_ref.at[pl.ds(layer, 1)], bu.at[:, pl.ds(0, ff)], bu.at[:, pl.ds(ff, ff)]),
-                          (wup_ref.at[layer], wu.at[:, pl.ds(0, ff)], wu.at[:, pl.ds(ff, ff)]),
-                          (wdown_ref.at[layer], wd.at[pl.ds(0, ff)], wd.at[pl.ds(ff, ff)])], wl, ws, wr)
-    place.greet()
-    for i in range(3):
-        share.load(i).start()
-    gather = Gather(place, buf, ag_send, ag_recv)
-
-    def norm(tile):
-        norm_rows(r_ref, norm_ref[layer, 2:3, :], norm_ref[layer, 3:4, :], buf, tile)
-
-    def share_all():
-        for i in range(3):
-            share.load(i).wait()
-            share.give(i).start()
-    gather.start(norm, lambda: None, share_all)
+
     scatter = Scatter(place, buf, r1, sums, mid, r2, s1_send, s1_recv, mid_send, mid_recv, s2_send, s2_recv)
     up_w, down_w = ff // 2, model // 4
+
     def up(j, c):
         rows = buf[pl.ds(2 * j, 2)].reshape(2 * block, model)
         cols = pl.ds(c * up_w, up_w)
@@ -508,22 +538,20 @@
         cols = pl.ds(c * down_w, down_w)
         buf[pl.ds(2 * j, 2), :, cols] = jnp.dot(u[...], wd[:, cols], preferred_element_type=F32).astype(BF16).reshape(2, block, down_w)
 
-    def send_slots(begin, end):
-        def one(slot, carry):
-            scatter.send_slot(slot)
-            return carry
-        lax.fori_loop(begin, end, one, 0)
-
-    def part(j, i):
+    def mlp_part(j, i):
         if i == 0:
             @pl.when(j == 0)
             def _():
-                share.give(0).wait_recv()
-                share.give(1).wait_recv()
+                share.load(6).wait()
+                pl.semaphore_wait(free, 1)
+                share.give(6).start()
+                share.give(4).wait_recv()
+                share.give(5).wait_recv()
 
             @pl.when(j == slots // 2 - 1)
             def _():
-                send_slots(0, slots - 2)
+                for d, dr in ((1, 1), (3, 0), (2, 0), (2, 1), (1, 0), (3, 1)):
+                    scatter.send_rows(d, dr, 0, slots - 2)
             up(j, 0)
             up(j, 1)
         elif i == 1:
@@ -533,19 +561,22 @@
         elif i == 3:
             @pl.when(j == 0)
             def _():
-                share.give(2).wait_recv()
-            gather.sent(2 * j)
-            gather.sent(2 * j + 1)
+                share.give(6).wait_recv()
+            gather2.sent(2 * j)
+            gather2.sent(2 * j + 1)
             down(j, 0)
         elif i == 4:
             down(j, 1)
         else:
             down(j, 2)
             down(j, 3)
-    gather.run(part)
-    send_slots(slots - 2, slots)
-    scatter.finish(r_ref, bias_ref[pl.ds(layer, 1), :], out_ref)
-    for i in range(3):
+    gather2.run(mlp_part)
+    for d, dr in ((1, 0), (3, 1)):
+        scatter.send_rows(d, dr, slots - 2, slots)
+    for dr in range(2):
+        scatter.send_rows(0, dr, 0, slots)
+    scatter.finish(res, bdown_ref[pl.ds(layer, 1), :], out_ref)
+    for i in (4, 5, 6):
         share.give(i).wait_send()
 
 
@@ -566,43 +597,22 @@
         residual = hidden_in.reshape(block, model)
         w_qkv = w_qkv.transpose(0, 2, 3, 1, 4).reshape(n_layers, 3, model, head_dim)
         w_out = w_out.reshape(n_layers, head_dim, model)
-        width = model // side
-        ring = [dma((2, chips - 1, subs))] * 2
-        rows = pltpu.VMEM((chips, block, model), BF16)
-
-        def params(collective_id):
-            return pltpu.CompilerParams(collective_id=collective_id, has_side_effects=True, vmem_limit_bytes=VMEM_LIMIT)
-
         for layer in range(n_layers):
             residual = pl.pallas_call(
-                functools.partial(attn_kernel, group_size, layer, n_seq), name=f"attn{layer}",
-                out_shape=jax.ShapeDtypeStruct((block, model), F32),
-                in_specs=[vmem, vmem, vmem, hbm, hbm], out_specs=vmem,
-                scratch_shapes=[rows, pltpu.VMEM((model, 6 * head_dim), BF16), pltpu.VMEM((2 * head_dim, model), BF16),
-                                pltpu.VMEM((chips, block, 6 * head_dim), BF16), pltpu.VMEM((chips, block, 4 * head_dim), BF16),
-                                pltpu.VMEM((n_chunks, chips, TILE, 2 * head_dim), BF16),
-                                pltpu.VMEM((side - 1, n_chunks, chips, TILE, 2 * head_dim), BF16),
-                                pltpu.VMEM((side - 1, 2 * head_dim, width), BF16),
-                                pltpu.VMEM((n_chunks, chips, TILE, width), BF16),
-                                pltpu.VMEM((side - 1, n_chunks, side, TILE, width), BF16),
-                                pltpu.VMEM((n_chunks, side, TILE, width), F32),
-                                pltpu.VMEM((side - 1, n_chunks, TILE, width), F32),
-                                dma((4,)), dma((4,)), dma((4,)), *ring, dma((chips // 2, 2)), dma((chips // 2, 2)),
-                                *[dma((n_chunks, side - 1))] * 2, *[dma((n_chunks, 2))] * 2, *[dma((side - 1, 2))] * 2,
-                                *[dma((n_chunks, side - 1))] * 4],
-                compiler_params=params(2 * layer),
-            )(residual, norms, b_out, w_qkv, w_out)
-            residual = pl.pallas_call(
-                functools.partial(mlp_kernel, group_size, layer), name=f"mlp{layer}",
+                functools.partial(layer_kernel, group_size, layer, n_seq), name=f"layer{layer}",
                 out_shape=jax.ShapeDtypeStruct((block, model), F32 if layer < n_layers - 1 else BF16),
-                in_specs=[vmem, vmem, vmem, hbm, hbm, hbm], out_specs=vmem,
-                scratch_shapes=[rows, pltpu.VMEM((model, 2 * ff), BF16), pltpu.VMEM((2 * ff, model), BF16), pltpu.VMEM((1, 2 * ff), F32),
-                                pltpu.VMEM((2 * block, 2 * ff), BF16), pltpu.VMEM((side - 1, side, block, model), BF16),
-                                pltpu.VMEM((side - 1, block, model), F32), pltpu.VMEM((block, model), F32),
-                                pltpu.VMEM((min(2, side - 1), block, model), F32), dma((3,)), dma((3,)), dma((3,)), *ring,
-                                *[dma((side - 1, side, 2))] * 2, *[dma((2, subs))] * 2, *[dma((2, 2, subs))] * 2],
-                compiler_params=params(2 * layer + 1),
-            )(residual, norms, b_down, b_up, w_up, w_down)
+                in_specs=[vmem] * 4 + [hbm] * 5, out_specs=vmem,
+                scratch_shapes=[
+                    pltpu.VMEM((chips, block, model), BF16), pltpu.VMEM((model, 2 * ff), BF16), pltpu.VMEM((2 * ff, model), BF16),
+                    pltpu.VMEM((1, 2 * ff), F32), pltpu.VMEM((2 * block, 2 * ff), BF16), pltpu.VMEM((side - 1, side, block, model), BF16),
+                    pltpu.VMEM((side - 1, block, model), F32), pltpu.VMEM((block, model), F32), pltpu.VMEM((2, block, model), F32),
+                    pltpu.VMEM((chips, block, 6 * head_dim), BF16), pltpu.VMEM((chips, block, 4 * head_dim), BF16),
+                    pltpu.VMEM((side - 1, 2 * head_dim, model // side), BF16), pltpu.VMEM((block, model), F32),
+                    *[dma((7,))] * 3, pltpu.SemaphoreType.REGULAR, *[dma((2, chips - 1, subs))] * 4, *[dma((chips // 2, 2))] * 2,
+                    *[dma((n_chunks, 2))] * 4, *[dma((side - 1, 2))] * 2, *[dma((n_chunks, side - 1))] * 4,
+                    *[dma((side - 1, side, 2))] * 2, *[dma((2, subs))] * 2, *[dma((2, 2, subs))] * 2],
+                compiler_params=pltpu.CompilerParams(collective_id=layer, has_side_effects=True, vmem_limit_bytes=VMEM_LIMIT),
+            )(residual, norms, b_out, b_down, b_up, w_qkv, w_out, w_up, w_down)
         return residual.reshape(n_seq, per_seq, model)
 
     in_specs = (P('dp', 'tp', None), P(), P(None, None, None, 'tp', None), P(None, 'tp', None, None), P(), P(None, None, 'tp'), P(None, 'tp'), P(None, 'tp', None), P())

time: 654 us -> 627 us (0.959)
  Pallas kernels: 651 us -> 624 us
    pallas_call x4 -> x2, Pallas kernels: 651 us -> 624 us  [local_layers(): pl.pallas_call(functools.partial(layer_kernel, group_size, layer, n_seq),...]
where the time goes in v3:
time: 627 us; the launch traced here: 626 us
  Pallas kernels  624 us (100%)
    pallas_call x2, Pallas kernels, local_layers(): pl.pallas_call(functools.partial(layer_kernel, group_size, layer, n_seq),...  624 us

profile of v3, /device:TPU:96, one launch (start us, length us, event | category | flops | bytes accessed | tf_op | source)
XLA Modules:
  0.0 626.1 jit_solution(18030448227176854360)
XLA Ops:
  0.0 313.3 %layer0.1.r_ref = f32[96,4096]{1,0:T(8,128)} custom-call(bf16[96,4096]{1,0:T(8,128)(2,1)} %bitcast.13, f32[2,4,4096]{2,1,0:T(4,128)} %norm_ref.3, f32[2,4096]{1,0:T(2,128)} %bout_ref.3, f32[2,4096]{1,0:T(2,128)} %bdown_ref.3, f32[2,512]{1,0:T(2,128)} %bup_ref.3, bf16[2,3,4096,128]{3,2,1,0:T(8,128)(2,1)} %bitcast.8, bf16[2,128,4096]{2,1,0:T(8,128)(2,1)} %bitcast.10, ...), custom_call_target="tpu_custom_call" | custom-call | tf_op jit(solution)/shard_map/layer0/pallas_call | solution.py:601
  313.4 310.7 %layer1.1 = bf16[96,4096]{1,0:T(8,128)(2,1)} custom-call(f32[96,4096]{1,0:T(8,128)} %layer0.1.r_ref, f32[2,4,4096]{2,1,0:T(4,128)} %norm_ref.3, f32[2,4096]{1,0:T(2,128)} %bout_ref.3, f32[2,4096]{1,0:T(2,128)} %bdown_ref.3, f32[2,512]{1,0:T(2,128)} %bup_ref.3, bf16[2,3,4096,128]{3,2,1,0:T(8,128)(2,1)} %bitcast.9, bf16[2,128,4096]{2,1,0:T(8,128)(2,1)} %bitcast.11, ...), custom_call_target="tpu_custom_call" | custom-call | tf_op jit(solution)/shard_map/layer1/pallas_call | solution.py:601
  624.1 2.1 copy.12

commit v4 on v0

v4 whole, which is shorter than its diff:
```python
import functools
import math

import jax
import jax.numpy as jnp
from jax import lax
from jax.experimental import pallas as pl
from jax.experimental.pallas import tpu as pltpu
from jax.sharding import PartitionSpec as P

LN_EPS = 1e-5
MESH = pl.DeviceIdType.MESH
F32 = jnp.float32
BF16 = jnp.bfloat16
VMEM_LIMIT = 66_900_000
TILE = 16


class Place:
    def __init__(self, group_size):
        self.side = side = math.isqrt(group_size // 2)
        self.chips = side * side
        index = lax.axis_index("tp")
        self.core = index % 2
        chip = index // 2
        x, y = chip % side, chip // side
        self.first = x * (1 - self.core) + y * self.core
        self.second = y * (1 - self.core) + x * self.core
        self.pos = self.pos_of(self.first, self.second)

    def device(self, first, second):
        x = first * (1 - self.core) + second * self.core
        y = second * (1 - self.core) + first * self.core
        return {"tp": (y * self.side + x) * 2 + self.core}

    def partner(self):
        x = self.first * (1 - self.core) + self.second * self.core
        y = self.second * (1 - self.core) + self.first * self.core
        return {"tp": (y * self.side + x) * 2 + 1 - self.core}

    def pos_of(self, first, second):
        return second * self.side + (first + second) % self.side

    def at_pos(self, pos):
        second = pos // self.side
        return (pos % self.side + self.side - second) % self.side, second

    def peers(self):
        peers = [self.device((self.first + d) % self.side, self.second) for d in range(1, self.side)]
        peers += [self.device(self.first, (self.second + d) % self.side) for d in range(1, self.side)]
        return [*peers, self.partner()]

    def greet(self):
        for peer in self.peers():
            pl.semaphore_signal(pltpu.get_barrier_semaphore(), inc=1, device_id=peer, device_id_type=MESH)

    def meet(self):
        pl.semaphore_wait(pltpu.get_barrier_semaphore(), 2 * self.side - 1)


def far_first(side):
    return sorted(range(1, side), key=lambda d: -min(d, side - d))


def remote(src, dst, send_sem, recv_sem, device):
    return pltpu.make_async_remote_copy(src_ref=src, dst_ref=dst, send_sem=send_sem, recv_sem=recv_sem, device_id=device, device_id_type=MESH)


def norm_rows(r_ref, gain, shift, buf, tile):
    rows = pl.ds(pl.multiple_of(tile * TILE, TILE), TILE)
    v = r_ref[rows, :].astype(F32)
    mean = jnp.mean(v, axis=-1, keepdims=True)
    v = v - mean
    var = jnp.mean(v * v, axis=-1, keepdims=True)
    buf[0, rows, :] = (v * lax.rsqrt(var + LN_EPS) * gain + shift).astype(BF16)


class Gather:
    def __init__(self, place, buf, send, recv):
        self.place, self.buf, self.send, self.recv = place, buf, send, recv
        self.half = buf.shape[1] // 2
        self.subs = self.half // TILE
        n = place.chips
        self.next = [place.device(*place.at_pos((place.pos + d) % n))["tp"] for d in (1, n - 1)]

    def hop(self, dr, s, k):
        rows = pl.ds(pl.multiple_of(dr * self.half + k * TILE, TILE), TILE)
        return remote(self.buf.at[s, rows], self.buf.at[s + 1, rows], self.send.at[dr, s, k], self.recv.at[dr, s, k],
                      {"tp": self.next[0] * (1 - dr) + self.next[1] * dr})

    def start(self, norm, before, meanwhile):
        norm(0)
        norm(self.subs)
        self.place.meet()
        before()

        def step(k, carry):
            norm(k)
            norm(self.subs + k)
            for dr in range(2):
                self.hop(dr, 0, k - 1).start()
            return carry
        lax.fori_loop(1, self.subs, step, 0)
        meanwhile()
        for dr in range(2):
            self.hop(dr, 0, self.subs - 1).start()

    def take(self, s, k):
        for dr in range(2):
            self.hop(dr, s - 1, k).wait_recv()

            @pl.when(s < self.place.chips - 1)
            def _():
                self.hop(dr, s, k).start()

    def sent(self, s):
        @pl.when(s < self.place.chips - 1)
        def _():
            for dr in range(2):
                for k in range(self.subs):
                    self.hop(dr, s, k).wait_send()

    def run(self, part):
        n = self.place.chips // 2
        for k in range(self.subs):
            self.take(1, k)

        def step(j, carry):
            for h in range(2):
                for k in range(self.subs):
                    @pl.when(j < n)
                    def _():
                        self.take(2 * j + h, k)
                    part(j - 1, h * self.subs + k)
            return carry
        lax.fori_loop(1, n + 1, step, 0)


class Scatter:
    def __init__(self, place, buf, r1, sums, mid, r2, s1_send, s1_recv, mid_send, mid_recv, s2_send, s2_recv):
        self.place, self.buf, self.r1, self.sums, self.mid, self.r2 = place, buf, r1, sums, mid, r2
        self.mid_send, self.mid_recv = mid_send, mid_recv
        self.s1_send, self.s1_recv, self.s2_send, self.s2_recv = s1_send, s1_recv, s2_send, s2_recv
        self.half = buf.shape[1] // 2

    def rows(self, dr):
        return pl.ds(dr * self.half, self.half)

    def first_copy(self, slot, dr, j, first, second):
        p = self.place
        return remote(self.buf.at[slot, self.rows(dr)], self.r1.at[j, second, self.rows(dr)], self.s1_send.at[j, second, dr],
                      self.s1_recv.at[j, second, dr], p.device(first, p.second))

    def send_rows(self, d, dr, begin, end):
        p = self.place
        second = (p.second + d) % p.side
        for away in far_first(p.side):
            first = (p.first + away) % p.side
            slot = self.slot_of(first, second, dr)

            @pl.when((slot >= begin) & (slot < end))
            def _():
                self.first_copy(slot, dr, p.side - 1 - away, first, second).start()

    def slot_of(self, first, second, dr):
        p = self.place
        pos = p.pos_of(first, second)
        return (p.pos + p.chips - pos) % p.chips if dr == 0 else (pos + p.chips - p.pos) % p.chips

    def arrived(self, second, dr):
        for j in range(self.place.side - 1):
            self.first_copy(0, dr, j, self.place.first, second).wait_recv()

    def total(self, second, dr, rows):
        v = self.buf[self.slot_of(self.place.first, second, dr), rows, :].astype(F32)
        for j in range(self.place.side - 1):
            v = v + self.r1[j, second, rows, :].astype(F32)
        return v

    def tile(self, dr, k):
        return pl.ds(pl.multiple_of(dr * self.half + k * TILE, TILE), TILE)

    def mid_copy(self, dr, k):
        p = self.place
        step = 1 if dr == 0 else p.side - 1
        rows = self.tile(dr, k)
        return remote(self.sums.at[1, rows], self.mid.at[rows], self.mid_send.at[dr, k], self.mid_recv.at[dr, k],
                      p.device(p.first, (p.second + step) % p.side))

    def end_copy(self, d, dr, k):
        p = self.place
        at = 0 if d == 1 else 1
        rows = self.tile(dr, k)
        return remote(self.sums.at[d - 1, rows], self.r2.at[at, rows], self.s2_send.at[at, dr, k], self.s2_recv.at[at, dr, k],
                      p.device(p.first, (p.second + d) % p.side))

    def add(self, d, dr, k, with_mid):
        second = (self.place.second + d) % self.place.side
        rows = self.tile(dr, k)
        v = self.total(second, dr, rows)
        if with_mid:
            self.mid_copy(dr, k).wait_recv()
            v = v + self.mid[rows, :]
        self.sums[d - 1, rows, :] = v

    def tiles(self, fn):
        def one(k, carry):
            fn(k)
            return carry
        lax.fori_loop(0, self.half // TILE, one, 0)

    def finish(self, res, bias, out_ref, meanwhile):
        p = self.place

        def pieces(group, with_mid, copy):
            for d, dr in group:
                self.arrived((p.second + d) % p.side, dr)

            def one(k):
                for d, dr in group:
                    self.add(d, dr, k, with_mid)
                    copy(d, dr, k).start()
            self.tiles(one)

        ends = [(1, 1), (p.side - 1, 0)] if p.side > 2 else [(1, 0), (1, 1)]
        pieces(ends, False, self.end_copy)
        if p.side > 2:
            pieces([(2, 0), (2, 1)], False, lambda d, dr, k: self.mid_copy(dr, k))
            more = [(1, 0), (p.side - 1, 1)]
            pieces(more, True, self.end_copy)
            ends = ends + more
        meanwhile()
        for dr in range(2):
            self.arrived(p.second, dr)

        def last(k):
            for dr in range(2):
                rows = self.tile(dr, k)
                for d, half in ends:
                    if half == dr:
                        self.end_copy(d, dr, k).wait_recv()
                v = self.total(p.second, dr, rows)
                for j in range(self.r2.shape[0]):
                    v = v + self.r2[j, rows, :]
                v = res[rows, :] + v + bias
                res[rows, :] = v
                out_ref[rows, :] = v.astype(out_ref.dtype)
        self.tiles(last)

        def sent(k):
            if p.side > 2:
                for dr in range(2):
                    self.mid_copy(dr, k).wait_send()
            for d, dr in ends:
                self.end_copy(d, dr, k).wait_send()
        self.tiles(sent)
        for dr in range(2):
            for j in range(p.side - 1):
                for second in range(p.side):
                    self.first_copy(0, dr, j, p.first, second).wait_send()


class Share:
    def __init__(self, place, pairs, local, send, recv):
        self.place, self.pairs, self.local, self.send, self.recv = place, pairs, local, send, recv

    def load(self, i):
        src, own, _ = self.pairs[i]
        return pltpu.make_async_copy(src, own, self.local.at[i])

    def give(self, i):
        _, own, other = self.pairs[i]
        return remote(own, other, self.send.at[i], self.recv.at[i], self.place.partner())


def layers_kernel(group_size, n_seq, r_ref, norm_ref, bout_ref, bdown_ref, bup_ref, wqkv_ref, wout_ref, wup_ref, wdown_ref, out_ref,
                 buf, wu, wd, bu, u, r1, sums, mid, r2, qkv, kvp, wo, w4, res,
                 wl, ws, wr, free, ag_send, ag_recv, ag2_send, ag2_recv, kv_send, kv_recv, a_send, a_recv, f_send, f_recv, w4_send, w4_recv,
                 p_send, p_recv, s_send, s_recv, s1_send, s1_recv, mid_send, mid_recv, s2_send, s2_recv):
    place = Place(group_size)
    slots, block, model = buf.shape
    side, hd, ff = place.side, w4.shape[1] // 2, wup_ref.shape[2]
    n_chunks, per_seq, width = block // TILE, block // n_seq, model // place.side
    per_row = side
    every = slots * TILE

    def widen(i, carry):
        rows = pl.ds(pl.multiple_of(i * TILE, TILE), TILE)
        res[rows, :] = r_ref[rows, :].astype(F32)
        return carry
    lax.fori_loop(0, n_chunks, widen, 0)

    def one_layer(layer, carry):
        share = Share(place, [(wout_ref.at[layer], wo.at[pl.ds(0, hd)], wo.at[pl.ds(hd, hd)])]
                      + [(wqkv_ref.at[layer, t], wu.at[:, pl.ds(t * hd, hd)], wu.at[:, pl.ds((3 + t) * hd, hd)]) for t in range(3)]
                      + [(bup_ref, bu.at[:, pl.ds(0, ff)], bu.at[:, pl.ds(ff, ff)]),
                         (wup_ref.at[layer], wu.at[:, pl.ds(0, ff)], wu.at[:, pl.ds(ff, ff)]),
                         (wdown_ref.at[layer], wd.at[pl.ds(0, ff)], wd.at[pl.ds(ff, ff)])], wl, ws, wr)
        area = [2 * hd + i * every for i in range(3)]

        def piece(i, n):
            return wd.at[pl.ds(area[i], every), pl.ds(pl.multiple_of(n * 2 * hd, 2 * hd), 2 * hd)]

        def heads(j, chunk):
            return (piece(2, chunk), piece(2, n_chunks + chunk), piece(1, n_chunks + chunk), piece(1, chunk))[j]

        def partial(chunk):
            over = chunk // per_row
            row = pl.multiple_of(area[0] + every * over * (chunk - per_row + 1), TILE)
            col = pl.multiple_of(width * (chunk * (1 - over) + (per_row - 1) * over), width)
            return row, pl.ds(col, width)

        def cell(chunk):
            return chunk // per_row, pl.ds(pl.multiple_of(chunk % per_row * width, width), width)

        place.greet()
        for i in range(1, 4):
            share.load(i).start()

        @pl.when(layer == 0)
        def _():
            share.load(0).start()
        gather = Gather(place, buf, ag_send, ag_recv)

        def norm(tile):
            norm_rows(res, norm_ref[layer, 0:1, :], norm_ref[layer, 1:2, :], buf, tile)

        def col(first):
            return pl.ds(pl.multiple_of(first * width, width), width)

        def w_copy(d, h):
            first = (place.first + d) % side
            rows = pl.ds(h * hd, hd)
            return remote(wo.at[rows, col(first)], w4.at[side - 1 - d, rows], w4_send.at[side - 1 - d, h], w4_recv.at[side - 1 - d, h],
                          place.device(first, place.second))

        def share_out(which):
            which.load(0).wait()
            which.give(0).start()
            for d in far_first(side):
                w_copy(d, 0).start()

        def share_rest(which):
            which.give(0).wait_recv()
            for d in far_first(side):
                w_copy(d, 1).start()

        def share_qkv():
            for i in range(1, 4):
                share.load(i).wait()
                share.give(i).start()
        gather.start(norm, lambda: pl.when(layer == 0)(lambda: share_out(share)), share_qkv)
        pl.when(layer == 0)(lambda: share_rest(share))

        def kv_copy(j, h):
            pair = pl.ds(2 * j, 2)
            return remote(qkv.at[pair, :, pl.ds(3 * hd * h + hd, 2 * hd)], kvp.at[pair, :, pl.ds(2 * hd * (1 - h), 2 * hd)],
                          kv_send.at[j, h], kv_recv.at[j, h], place.partner())

        def qkv_part(j, i):
            if i % 2 == 0:
                if i == 0:
                    @pl.when(j == 0)
                    def _():
                        for t in range(3):
                            share.give(1 + t).wait_recv()
                cols = pl.ds(i // 2 * 2 * hd, 2 * hd)
                rows = buf[pl.ds(2 * j, 2)].reshape(2 * block, model)
                qkv[pl.ds(2 * j, 2), :, cols] = jnp.dot(rows, wu[:, cols], preferred_element_type=F32).astype(BF16).reshape(2, block, 2 * hd)
            if i == 5:
                for h in range(2):
                    kv_copy(j, h).start()
                gather.sent(2 * j)
                gather.sent(2 * j + 1)
        gather.run(qkv_part)
        for j in range(slots // 2):
            for h in range(2):
                kv_copy(j, h).wait_recv()
        for i in range(1, 4):
            share.give(i).wait_send()
        for i in (4, 5):
            share.load(i).start()

        nk = slots * per_seq

        def rows_of(chunk):
            return pl.ds(pl.multiple_of(chunk * TILE, TILE), TILE)

        def attend(chunk):
            seq = chunk * TILE // per_seq
            lower = chunk * TILE // (block // 2)
            keys = pl.ds(pl.multiple_of(seq * per_seq, per_seq), per_seq)

            def head_of(h, carry):
                def cols(base, k):
                    return pl.ds(pl.multiple_of(h * base + k * hd, hd), hd)
                q = qkv[:, rows_of(chunk), cols(3 * hd, 0)].reshape(every, hd)
                k0 = qkv[:, keys, cols(3 * hd, 1)].reshape(nk, hd)
                v0 = qkv[:, keys, cols(3 * hd, 2)].reshape(nk, hd)
                k1 = kvp[:, keys, cols(2 * hd, 0)].reshape(nk, hd)
                v1 = kvp[:, keys, cols(2 * hd, 1)].reshape(nk, hd)
                dims = (((1,), (1,)), ((), ()))
                s0 = lax.dot_general(q, k0, dims, preferred_element_type=F32) * hd ** -0.5
                s1 = lax.dot_general(q, k1, dims, preferred_element_type=F32) * hd ** -0.5
                top = jnp.maximum(jnp.max(s0, axis=-1, keepdims=True), jnp.max(s1, axis=-1, keepdims=True))
                e0 = jnp.exp(s0 - top)
                e1 = jnp.exp(s1 - top)
                inv = 1.0 / (jnp.sum(e0, axis=-1, keepdims=True) + jnp.sum(e1, axis=-1, keepdims=True))
                a = jnp.dot((e0 * inv).astype(BF16), v0, preferred_element_type=F32)
                a = (a + jnp.dot((e1 * inv).astype(BF16), v1, preferred_element_type=F32)).astype(BF16)
                for slot in range(slots):
                    pos = (place.pos + (slots - slot) * (1 - lower) + slot * lower) % slots
                    wd[pl.ds(pl.multiple_of(area[1] + pos * TILE, TILE), TILE),
                       pl.ds(pl.multiple_of(chunk * 2 * hd + h * hd, hd), hd)] = a[slot * TILE:(slot + 1) * TILE]
                return carry
            lax.fori_loop(0, 2, head_of, 0)
            for d in near:
                a_copy(chunk, d).start()

        near = (1, side - 1)

        def a_copy(chunk, d):
            return remote(heads(side - 1, chunk), heads(side - 1 - d, chunk), a_send.at[chunk, d // 2], a_recv.at[chunk, d // 2],
                          place.device((place.first + d) % side, place.second))

        def f_copy(chunk, h):
            cols = pl.ds(h * hd, hd)
            return remote(heads(2 - 2 * h, chunk).at[:, cols], heads(1, chunk).at[:, cols], f_send.at[chunk, h], f_recv.at[chunk, h],
                          place.device((place.first + (1 if h == 0 else side - 1)) % side, place.second))

        def forward(chunk):
            for d in near:
                a_copy(chunk, d).wait_recv()
            for h in range(2):
                f_copy(chunk, h).start()

            @pl.when(chunk == 0)
            def _():
                for i in (4, 5):
                    share.load(i).wait()
                    share.give(i).start()

        def p_copy(chunk, d):
            second = (place.second + d) % side
            row, cols = partial(chunk)
            at, there = cell(chunk)
            return remote(wd.at[pl.ds(pl.multiple_of(row + second * side * TILE, TILE), side * TILE), cols],
                          r1.at[side - 1 - d, at, pl.ds(0, side * TILE), there], p_send.at[chunk, side - 1 - d], p_recv.at[chunk, side - 1 - d],
                          place.device(place.first, second))

        def project(chunk):
            @pl.when(chunk == 0)
            def _():
                for d in range(1, side):
                    for h in range(2):
                        w_copy(d, h).wait_recv()
            for h in range(2):
                f_copy(chunk, h).wait_recv()
            half = width // 2
            row, cols = partial(chunk)
            for c in range(2):
                own = pl.ds(pl.multiple_of(place.first * width + c * half, half), half)
                v = jnp.dot(heads(side - 1, chunk)[...], wo[:, own], preferred_element_type=F32)
                for j in range(side - 1):
                    v = v + jnp.dot(heads(j, chunk)[...], w4[j, :, pl.ds(c * half, half)], preferred_element_type=F32)
                wd[pl.ds(row, every), pl.ds(pl.multiple_of(cols.start + c * half, half), half)] = v.astype(BF16)
            for d in far_first(side):
                p_copy(chunk, d).start()

        def s_copy(chunk, d):
            first = (place.first + d) % side
            at, there = cell(chunk)
            i = (first + place.second) % side
            return remote(sums.at[at, pl.ds(pl.multiple_of(i * TILE, TILE), TILE), there],
                          r2.at[0, rows_of(chunk), pl.ds((side - 1 - d) * width, width)], s_send.at[chunk, side - 1 - d], s_recv.at[chunk, side - 1 - d],
                          place.device(first, place.second))

        def add(chunk):
            for d in range(1, side):
                p_copy(chunk, d).wait_recv()
            row, cols = partial(chunk)
            at, there = cell(chunk)

            def one(i, carry):
                rows = rows_of(i)
                v = wd[pl.ds(pl.multiple_of(row + (place.second * side + i) * TILE, TILE), TILE), cols].astype(F32)
                for j in range(side - 1):
                    v = v + r1[j, at, rows, there].astype(F32)
                sums[at, rows, there] = v
                return carry
            lax.fori_loop(0, side, one, 0)
            for d in far_first(side):
                s_copy(chunk, d).start()

        gather2 = Gather(place, buf, ag2_send, ag2_recv)
        subs = gather2.subs

        def output(chunk):
            rows = rows_of(chunk)
            at, there = cell(chunk)

            def put(first, v):
                res[rows, col(first)] = res[rows, col(first)] + v + bout_ref[pl.ds(layer, 1), col(first)]
            put(place.first, sums[at, pl.ds(pl.multiple_of((place.first + place.second) % side * TILE, TILE), TILE), there])
            for j in range(side - 1):
                s_copy(chunk, side - 1 - j).wait_recv()
                put((place.first + 1 + j) % side, r2[0, rows, pl.ds(j * width, width)])
            norm_rows(res, norm_ref[layer, 2:3, :], norm_ref[layer, 3:4, :], buf, chunk)

            @pl.when(chunk > 0)
            def _():
                gather2.hop((chunk - 1) // subs, 0, (chunk - 1) % subs).start()

        lag = n_chunks // 2
        stages = ((attend, 0), (forward, lag - 1), (project, lag), (add, lag + 1), (output, lag + 2))

        def step(i, carry):
            for stage, at in stages:
                @pl.when((i >= at) & (i < at + n_chunks))
                def _():
                    stage(i - at)
            return carry
        lax.fori_loop(0, n_chunks + lag + 2, step, 0)

        def done(chunk, carry):
            for d in range(1, side):
                p_copy(chunk, d).wait_send()
                s_copy(chunk, d).wait_send()
            for d in near:
                a_copy(chunk, d).wait_send()
            for h in range(2):
                f_copy(chunk, h).wait_send()
            return carry
        lax.fori_loop(0, n_chunks, done, 0)
        gather2.hop(1, 0, subs - 1).start()
        for d in range(1, side):
            for h in range(2):
                w_copy(d, h).wait_send()
        share.give(0).wait_send()
        share.load(6).start()
        pl.semaphore_signal(free, inc=1, device_id=place.partner(), device_id_type=MESH)
        for j in range(slots // 2):
            for h in range(2):
                kv_copy(j, h).wait_send()

        scatter = Scatter(place, buf, r1, sums, mid, r2, s1_send, s1_recv, mid_send, mid_recv, s2_send, s2_recv)
        up_w, down_w = ff // 2, model // 4

        def up(j, c):
            rows = buf[pl.ds(2 * j, 2)].reshape(2 * block, model)
            cols = pl.ds(c * up_w, up_w)
            hidden = jnp.dot(rows, wu[:, cols], preferred_element_type=F32) + bu[pl.ds(layer, 1), cols]
            u[:, cols] = jax.nn.gelu(hidden, approximate=True).astype(BF16)

        def down(j, c):
            cols = pl.ds(c * down_w, down_w)
            buf[pl.ds(2 * j, 2), :, cols] = jnp.dot(u[...], wd[:, cols], preferred_element_type=F32).astype(BF16).reshape(2, block, down_w)

        def mlp_part(j, i):
            if i == 0:
                @pl.when(j == 0)
                def _():
                    share.load(6).wait()
                    pl.semaphore_wait(free, 1)
                    share.give(6).start()
                    share.give(4).wait_recv()
                    share.give(5).wait_recv()

                @pl.when(j == slots // 2 - 1)
                def _():
                    for d, dr in ((1, 1), (3, 0), (2, 0), (2, 1), (1, 0), (3, 1)):
                        scatter.send_rows(d, dr, 0, slots - 2)
                up(j, 0)
                up(j, 1)
            elif i == 1:
                up(j, 2)
            elif i == 2:
                up(j, 3)
            elif i == 3:
                @pl.when(j == 0)
                def _():
                    share.give(6).wait_recv()
                gather2.sent(2 * j)
                gather2.sent(2 * j + 1)
                down(j, 0)
            elif i == 4:
                down(j, 1)
            else:
                down(j, 2)
                down(j, 3)
        gather2.run(mlp_part)
        for d, dr in ((1, 0), (3, 1)):
            scatter.send_rows(d, dr, slots - 2, slots)
        for dr in range(2):
            scatter.send_rows(0, dr, 0, slots)
        following = Share(place, [(wout_ref.at[layer + 1], wo.at[pl.ds(0, hd)], wo.at[pl.ds(hd, hd)])], wl, ws, wr)
        more = pl.when(layer + 1 < wqkv_ref.shape[0])
        more(lambda: following.load(0).start())
        scatter.finish(res, bdown_ref[pl.ds(layer, 1), :], out_ref, lambda: more(lambda: share_out(following)))
        more(lambda: share_rest(following))
        for i in (4, 5, 6):
            share.give(i).wait_send()
        return carry
    lax.fori_loop(0, wqkv_ref.shape[0], one_layer, 0)


def solution(mesh):
    group_size = mesh.shape["tp"]
    side = math.isqrt(group_size // 2)
    chips = side * side
    dma = pltpu.SemaphoreType.DMA
    vmem = pl.BlockSpec(memory_space=pltpu.VMEM)
    hbm = pl.BlockSpec(memory_space=pl.ANY)

    def local_layers(hidden_in, norms, w_qkv, w_out, b_out, w_up, b_up, w_down, b_down):
        n_seq, per_seq, model = hidden_in.shape
        n_layers, head_dim, ff = w_qkv.shape[0], w_qkv.shape[-1], w_up.shape[-1]
        block = n_seq * per_seq
        subs = block // 2 // TILE
        n_chunks = block // TILE
        residual = hidden_in.reshape(block, model)
        w_qkv = w_qkv.transpose(0, 2, 3, 1, 4).reshape(n_layers, 3, model, head_dim)
        w_out = w_out.reshape(n_layers, head_dim, model)
        residual = pl.pallas_call(
            functools.partial(layers_kernel, group_size, n_seq), name="layers",
            out_shape=jax.ShapeDtypeStruct((block, model), BF16),
            in_specs=[vmem] * 4 + [hbm] * 5, out_specs=vmem,
            scratch_shapes=[
                pltpu.VMEM((chips, block, model), BF16), pltpu.VMEM((model, 2 * ff), BF16), pltpu.VMEM((2 * ff, model), BF16),
                pltpu.VMEM((n_layers, 2 * ff), F32), pltpu.VMEM((2 * block, 2 * ff), BF16), pltpu.VMEM((side - 1, side, block, model), BF16),
                pltpu.VMEM((side - 1, block, model), F32), pltpu.VMEM((block, model), F32), pltpu.VMEM((2, block, model), F32),
                pltpu.VMEM((chips, block, 6 * head_dim), BF16), pltpu.VMEM((chips, block, 4 * head_dim), BF16),
                pltpu.VMEM((2 * head_dim, model), BF16), pltpu.VMEM((side - 1, 2 * head_dim, model // side), BF16),
                pltpu.VMEM((block, model), F32),
                *[dma((7,))] * 3, pltpu.SemaphoreType.REGULAR, *[dma((2, chips - 1, subs))] * 4, *[dma((chips // 2, 2))] * 2,
                *[dma((n_chunks, 2))] * 4, *[dma((side - 1, 2))] * 2, *[dma((n_chunks, side - 1))] * 4,
                *[dma((side - 1, side, 2))] * 2, *[dma((2, subs))] * 2, *[dma((2, 2, subs))] * 2],
            compiler_params=pltpu.CompilerParams(collective_id=0, has_side_effects=True, vmem_limit_bytes=VMEM_LIMIT),
        )(residual, norms, b_out, b_down, b_up, w_qkv, w_out, w_up, w_down)
        return residual.reshape(n_seq, per_seq, model)

    in_specs = (P('dp', 'tp', None), P(), P(None, None, None, 'tp', None), P(None, 'tp', None, None), P(), P(None, None, 'tp'), P(None, 'tp'), P(None, 'tp', None), P())
    return jax.shard_map(local_layers, mesh=mesh, in_specs=in_specs, out_specs=P('dp', 'tp', None), check_vma=False)
```

time: 2550 us -> 614 us (0.24); the launches traced: 2510 us -> 614 us
  waiting for transfers between devices: 1270 us -> 0 us
  blocking collectives: 807 us -> 0 us
  Pallas kernels: 0 us -> 612 us
  matrix products: 180 us -> 0 us
  local copies, waits for them, and re-layouts: 147 us -> 2.06 us
  other arithmetic: 89 us -> 0 us
    all_to_all x2 -> x0, waiting for transfers between devices: 830 us -> none  [reduce_rows(): lax.all_to_all(partial.astype(jnp.bfloat16), 'tp', 1, 0, tiled=True)]
    all_to_all x2 -> x0, blocking collectives: 807 us -> none  [reduce_rows(): lax.all_to_all(partial.astype(jnp.bfloat16), 'tp', 1, 0, tiled=True)]
    pallas_call x0 -> x1, Pallas kernels: none -> 612 us  [local_layers(): pl.pallas_call(functools.partial(layers_kernel, group_size, n_seq), name=...]
    all_gather x4 -> x0, waiting for transfers between devices: 436 us -> none  [the longest x2 223 us: local_layers(): full_rows2 = lax.all_gather(normed2, 'tp', axis=1, tiled=True)]
    dot_general x8 -> x0, matrix products: 160 us -> none  [the longest x2 44.3 us: local_layers(): jnp.einsum('bsd,df->bsf', full_rows2, w_up[layer_idx], preferred_element_...]
    convert_element_type x4 -> x0, local copies, waits for them, and re-layouts: 143 us -> none  [reduce_rows(): partial.astype(jnp.bfloat16)]
    reduce_sum x12 -> x0, other arithmetic: 79.6 us -> none  [the longest x4 67.8 us: reduce_rows(): return jnp.sum(received.astype(jnp.float32), axis=0)]
  transfers between devices with their start and end apart: 6 -> 0, of which waited for: 6 -> 0; matrix products, arithmetic and copies ran while one was open for 0% -> 0% of each run, Pallas kernels for 0% -> 0%
where the time goes in v4:
time: 614 us
  Pallas kernels  612 us (100%)
    pallas_call x1, Pallas kernels, local_layers(): pl.pallas_call(functools.partial(layers_kernel, group_size, n_seq), name=...  612 us

profile of v4, /device:TPU:96, one launch (start us, length us, event | category | flops | bytes accessed | tf_op | source)
XLA Modules:
  0.0 613.8 jit_solution(6314616150298041756)
XLA Ops:
  0.0 611.7 %layers.1 = bf16[96,4096]{1,0:T(8,128)(2,1)} custom-call(bf16[96,4096]{1,0:T(8,128)(2,1)} %bitcast.11, f32[2,4,4096]{2,1,0:T(4,128)} %norm_ref.1, f32[2,4096]{1,0:T(2,128)} %bout_ref.1, f32[2,4096]{1,0:T(2,128)} %bdown_ref.1, f32[2,512]{1,0:T(2,128)} %bup_ref.1, bf16[2,3,4096,128]{3,2,1,0:T(8,128)(2,1)} %bitcast.8, bf16[2,128,4096]{2,1,0:T(8,128)(2,1)} %bitcast.10, ...), custom_call_target="tpu_custom_call" | custom-call | tf_op jit(solution)/shard_map/layers/pallas_call | solution.py:624
  611.7 2.1 copy.12

commit v5 on v4

--- a/solution.py
+++ b/solution.py
@@ -334,9 +334,11 @@
             return remote(wo.at[rows, col(first)], w4.at[side - 1 - d, rows], w4_send.at[side - 1 - d, h], w4_recv.at[side - 1 - d, h],
                           place.device(first, place.second))
 
-        def share_out(which):
+        def share_own(which):
             which.load(0).wait()
             which.give(0).start()
+
+        def share_out(which):
             for d in far_first(side):
                 w_copy(d, 0).start()
 
@@ -349,7 +351,7 @@
             for i in range(1, 4):
                 share.load(i).wait()
                 share.give(i).start()
-        gather.start(norm, lambda: pl.when(layer == 0)(lambda: share_out(share)), share_qkv)
+        gather.start(norm, lambda: pl.when(layer == 0)(lambda: (share_own(share), share_out(share))[1]), share_qkv)
         pl.when(layer == 0)(lambda: share_rest(share))
 
         def kv_copy(j, h):
@@ -568,8 +570,13 @@
 
                 @pl.when(j == slots // 2 - 1)
                 def _():
-                    for d, dr in ((1, 1), (3, 0), (2, 0), (2, 1), (1, 0), (3, 1)):
+                    for d, dr in ((2, 0), (2, 1), (1, 0), (3, 1)):
                         scatter.send_rows(d, dr, 0, slots - 2)
+
+                @pl.when(j == slots // 2 - 3)
+                def _():
+                    for d, dr in ((1, 1), (3, 0)):
+                        scatter.send_rows(d, dr, 0, slots // 2)
                 up(j, 0)
                 up(j, 1)
             elif i == 1:
@@ -596,8 +603,8 @@
         following = Share(place, [(wout_ref.at[layer + 1], wo.at[pl.ds(0, hd)], wo.at[pl.ds(hd, hd)])], wl, ws, wr)
         more = pl.when(layer + 1 < wqkv_ref.shape[0])
         more(lambda: following.load(0).start())
-        scatter.finish(res, bdown_ref[pl.ds(layer, 1), :], out_ref, lambda: more(lambda: share_out(following)))
-        more(lambda: share_rest(following))
+        more(lambda: share_own(following))
+        scatter.finish(res, bdown_ref[pl.ds(layer, 1), :], out_ref, lambda: more(lambda: (share_out(following), share_rest(following))[1]))
         for i in (4, 5, 6):
             share.give(i).wait_send()
         return carry

time: 614 us -> 617 us (level)
  no operation moved by 1% of the time
where the time goes in v5:
time: 617 us; the launch traced here: 616 us
  Pallas kernels  614 us (100%)
    pallas_call x1, Pallas kernels, local_layers(): pl.pallas_call(functools.partial(layers_kernel, group_size, n_seq), name=...  614 us

profile of v5, /device:TPU:96, one launch (start us, length us, event | category | flops | bytes accessed | tf_op | source)
XLA Modules:
  0.0 616.0 jit_solution(6169336746923524259)
XLA Ops:
  0.0 614.0 %layers.1 = bf16[96,4096]{1,0:T(8,128)(2,1)} custom-call(bf16[96,4096]{1,0:T(8,128)(2,1)} %bitcast.11, f32[2,4,4096]{2,1,0:T(4,128)} %norm_ref.1, f32[2,4096]{1,0:T(2,128)} %bout_ref.1, f32[2,4096]{1,0:T(2,128)} %bdown_ref.1, f32[2,512]{1,0:T(2,128)} %bup_ref.1, bf16[2,3,4096,128]{3,2,1,0:T(8,128)(2,1)} %bitcast.8, bf16[2,128,4096]{2,1,0:T(8,128)(2,1)} %bitcast.10, ...), custom_call_target="tpu_custom_call" | custom-call | tf_op jit(solution)/shard_map/layers/pallas_call | solution.py:631
  614.0 2.1 copy.12
